TPU v7x, 128 devices: a whole 4x4x4 slice. The times are simulated.
128 devices in a mesh: lat: 8 (over z, x_hi), lon: 16 (over y, x_lo, core).
Axes of the slice: x: 4 (x_hi: 2, x_lo: 2; x = x_hi * 2 + x_lo), y: 4, z: 4, core: 2. Of those that a mesh axis runs over, the one named last changes fastest.
Arguments:
- fine_field: bfloat16 [128, 768, 128], P('lat', 'lon'), may hold values from -6 to 6
- w_enc: bfloat16 [3, 3, 128, 128], replicated, may hold values from -0.1875 to 0.1875
- w_down: bfloat16 [128, 512], replicated, may hold values from -0.5 to 0.5
- w_bot: bfloat16 [3, 3, 512, 512], replicated, may hold values from -0.09375 to 0.09375
- w_up: bfloat16 [512, 128], replicated, may hold values from -0.25 to 0.25
- w_dec: bfloat16 [3, 3, 128, 128], replicated, may hold values from -0.1875 to 0.1875
- out_grad: bfloat16 [128, 768, 128], P('lat', 'lon'), may hold values from -6 to 6
Outputs:
- block_out: bfloat16 [128, 768, 128], P('lat', 'lon')
- field_grad: bfloat16 [128, 768, 128], P('lat', 'lon')
- g_enc: float32 [3, 3, 128, 128], replicated
- g_down: float32 [128, 512], replicated
- g_bot: float32 [3, 3, 512, 512], replicated
- g_up: float32 [512, 128], replicated
- g_dec: float32 [3, 3, 128, 128], replicated
All inputs are finite; a program needn't handle non-finite values.
Results may differ from a plain program's by a relative error of at most 0.015.
Values may be sent and summed in bfloat16 or wider, within the bound.
No kernel may reach another device: no remote copies, remote signals or barrier semaphores. Data moves between devices by JAX's collectives and lax.ppermute only.
A program may use at most 128 MiB of HBM per device.

v0:
```python
import jax
import jax.numpy as jnp
from jax import lax
from jax.sharding import PartitionSpec as P

POOL = 8


def padded(block, sides, width, periodic):
    for axis, dim in sides:
        count = lax.axis_size(axis)
        forward = [(i, i + 1) for i in range(count - 1)]
        if periodic:
            forward.append((count - 1, 0))
        backward = [(target, source) for source, target in forward]
        low = lax.ppermute(
            lax.slice_in_dim(block, block.shape[dim] - width, None, axis=dim), axis, forward
        )
        high = lax.ppermute(lax.slice_in_dim(block, 0, width, axis=dim), axis, backward)
        block = jnp.concatenate([low, block, high], axis=dim)
    return block


def with_rim(field):
    widened = padded(field, (("lon", 1),), 1, True)
    return padded(widened, (("lat", 0),), 1, False)


def tile_viewer(extended, height, breadth):

    def viewer(down, across):
        return extended[1 + down : 1 + down + height, 1 + across : 1 + across + breadth]

    return viewer


def conv_fwd(viewer, kernel, height, breadth):
    total = jnp.zeros((height * breadth, kernel.shape[3]), jnp.float32)
    for tap_a in range(3):
        for tap_b in range(3):
            view = viewer(tap_a - 1, tap_b - 1).reshape(-1, kernel.shape[2])
            total = total + jnp.dot(view, kernel[tap_a, tap_b], preferred_element_type=jnp.float32)
    return total.reshape(height, breadth, kernel.shape[3])


def conv_back(viewer, kernel, height, breadth):
    total = jnp.zeros((height * breadth, kernel.shape[2]), jnp.float32)
    for tap_a in range(3):
        for tap_b in range(3):
            view = viewer(1 - tap_a, 1 - tap_b).reshape(-1, kernel.shape[3])
            total = total + jnp.dot(
                view, kernel[tap_a, tap_b].T, preferred_element_type=jnp.float32
            )
    return total.reshape(height, breadth, kernel.shape[2])


def cross(left, right):
    return lax.dot_general(
        left.reshape(-1, left.shape[-1]),
        right.reshape(-1, right.shape[-1]),
        (((0,), (0,)), ((), ())),
        preferred_element_type=jnp.float32,
    )


def kernel_grad(viewer, grad):
    rows_out = []
    for tap_a in range(3):
        row_list = []
        for tap_b in range(3):
            row_list.append(cross(viewer(tap_a - 1, tap_b - 1), grad))
        rows_out.append(jnp.stack(row_list))
    return jnp.stack(rows_out)


def mapped(field, matrix):
    flat = jnp.dot(field.reshape(-1, field.shape[-1]), matrix, preferred_element_type=jnp.float32)
    return flat.reshape(field.shape[:-1] + (matrix.shape[1],))


def slope(value):
    sig = jax.nn.sigmoid(value)
    return sig * (1.0 + value * (1.0 - sig))


def block_total(field):
    height, breadth, depth = field.shape
    return (
        field.astype(jnp.float32)
        .reshape(height // POOL, POOL, breadth // POOL, POOL, depth)
        .sum(axis=(1, 3))
    )


def repeated(field):
    height, breadth, depth = field.shape
    wide = jnp.broadcast_to(field[:, None, :, None, :], (height, POOL, breadth, POOL, depth))
    return wide.reshape(height * POOL, breadth * POOL, depth)


def body(fine_field, w_enc, w_down, w_bot, w_up, w_dec, out_grad):
    height, breadth, depth = fine_field.shape
    crow = height // POOL
    ccol = breadth // POOL
    fine_view = tile_viewer(with_rim(fine_field), height, breadth)
    act = conv_fwd(fine_view, w_enc, height, breadth)
    hid = jax.nn.silu(act).astype(jnp.bfloat16)
    pooled = (block_total(hid) / (POOL * POOL)).astype(jnp.bfloat16)
    coarse = mapped(pooled, w_down).astype(jnp.bfloat16)
    coarse_view = tile_viewer(with_rim(coarse), crow, ccol)
    zpre = conv_fwd(coarse_view, w_bot, crow, ccol)
    zact = jax.nn.silu(zpre).astype(jnp.bfloat16)
    lifted = mapped(zact, w_up)
    merged = (hid.astype(jnp.float32) + repeated(lifted)).astype(jnp.bfloat16)
    merged_view = tile_viewer(with_rim(merged), height, breadth)
    block_out = conv_fwd(merged_view, w_dec, height, breadth).astype(jnp.bfloat16)
    grad_view = tile_viewer(with_rim(out_grad), height, breadth)
    dmerged = conv_back(grad_view, w_dec, height, breadth)
    g_dec = kernel_grad(merged_view, out_grad)
    dlift = block_total(dmerged).astype(jnp.bfloat16)
    g_up = cross(zact, dlift)
    dzpre = (mapped(dlift, w_up.T) * slope(zpre)).astype(jnp.bfloat16)
    g_bot = kernel_grad(coarse_view, dzpre)
    dz_view = tile_viewer(with_rim(dzpre), crow, ccol)
    dcoarse = conv_back(dz_view, w_bot, crow, ccol).astype(jnp.bfloat16)
    g_down = cross(pooled, dcoarse)
    dpool = mapped(dcoarse, w_down.T)
    dact = ((dmerged + repeated(dpool) / (POOL * POOL)) * slope(act)).astype(jnp.bfloat16)
    dact_view = tile_viewer(with_rim(dact), height, breadth)
    field_grad = conv_back(dact_view, w_enc, height, breadth).astype(jnp.bfloat16)
    g_enc = kernel_grad(fine_view, dact)
    g_enc, g_down, g_bot, g_up, g_dec = lax.psum(
        (g_enc, g_down, g_bot, g_up, g_dec), ("lat", "lon")
    )
    return (block_out, field_grad, g_enc, g_down, g_bot, g_up, g_dec)


def solution(mesh):
    return jax.shard_map(
        body,
        mesh=mesh,
        in_specs=(P("lat", "lon", None), P(), P(), P(), P(), P(), P("lat", "lon", None)),
        out_specs=(P("lat", "lon", None), P("lat", "lon", None), P(), P(), P(), P(), P()),
        check_vma=False,
    )
```

profile of v0, /device:TPU:1, one launch (start us, length us, event | category | flops | bytes accessed | tf_op | source)
XLA Modules:
  0.0 336.3 jit_solution(11163730185095978388)
XLA Ops:
  8.1 2.7 collective-permute-start.12
  11.6 1.8 collective-permute-start
  17.4 4.8 %collective-permute-start.2 = (bf16[1,50,128]{2,1,0:T(8,128)(2,1)S(1)}, bf16[1,50,128]{2,1,0:T(8,128)(2,1)S(1)}, u32[]{:S(2)}, u32[]{:S(2)}) collective-permute-start(bf16[1,50,128]{2,1,0:T(8,128)(2,1)S(1)} %get-tuple-element.54), channel_id=1, source_target_pairs={{0,16},{16,32},{32,48},{48,64},{64,80},{80,96},{96,112},{1,17},{17... | collective-permute-start | bytes 38408 | tf_op jit(solution)/shard_map/ppermute | solution.py:16
  25.5 6.1 %collective-permute-start.15 = (bf16[1,50,128]{2,1,0:T(8,128)(2,1)S(1)}, bf16[1,50,128]{2,1,0:T(8,128)(2,1)S(1)}, u32[]{:S(2)}, u32[]{:S(2)}) collective-permute-start(bf16[1,50,128]{2,1,0:T(8,128)(2,1)S(1)} %get-tuple-element.47), channel_id=1, source_target_pairs={{0,16},{16,32},{32,48},{48,64},{64,80},{80,96},{96,112},{1,17},{17... | collective-permute-start | bytes 38408 | tf_op jit(solution)/shard_map/ppermute | solution.py:16
  39.2 4.1 %collective-permute-start.5 = (bf16[2,1,512]{2,1,0:T(2,128)(2,1)S(1)}, bf16[2,1,512]{2,1,0:T(2,128)(2,1)S(1)}, u32[]{:S(2)}, u32[]{:S(2)}) collective-permute-start(bf16[2,1,512]{2,1,0:T(2,128)(2,1)S(1)} %get-tuple-element.99), channel_id=1, source_target_pairs={{1,0},{2,1},{3,2},{4,3},{5,4},{6,5},{7,6},{8,7},{9,8},{10,9},{11,1... | collective-permute-start | bytes 6152 | tf_op jit(solution)/shard_map/ppermute | solution.py:19
  46.0 6.0 %collective-permute-start.6 = (bf16[1,8,512]{2,1,0:T(8,128)(2,1)S(1)}, bf16[1,8,512]{2,1,0:T(8,128)(2,1)S(1)}, u32[]{:S(2)}, u32[]{:S(2)}) collective-permute-start(bf16[1,8,512]{2,1,0:T(8,128)(2,1)S(1)} %get-tuple-element.96), channel_id=1, source_target_pairs={{0,16},{16,32},{32,48},{48,64},{64,80},{80,96},{96,112},{1,17},{17... | collective-permute-start | bytes 24584 | tf_op jit(solution)/shard_map/ppermute | solution.py:16
  53.4 4.5 %collective-permute-done.7 = bf16[1,8,512]{2,1,0:T(8,128)(2,1)S(1)} collective-permute-done((bf16[1,8,512]{2,1,0:T(8,128)(2,1)S(1)}, bf16[1,8,512]{2,1,0:T(8,128)(2,1)S(1)}, u32[]{:S(2)}, u32[]{:S(2)}) %collective-permute-start.7) | collective-permute-done | bytes 8224 | tf_op jit(solution)/shard_map/ppermute | solution.py:19
  66.7 1.9 multiply_convert_fusion.5
  73.3 1.3 convolution_bitcast_fusion.2
  75.9 1.4 convolution_bitcast_fusion.6
  80.9 5.5 %collective-permute-start.17 = (bf16[2,1,512]{2,1,0:T(2,128)(2,1)}, bf16[2,1,512]{2,1,0:T(2,128)(2,1)S(1)}, u32[]{:S(2)}, u32[]{:S(2)}) collective-permute-start(bf16[2,1,512]{2,1,0:T(2,128)(2,1)} %get-tuple-element.93), channel_id=1, source_target_pairs={{1,0},{2,1},{3,2},{4,3},{5,4},{6,5},{7,6},{8,7},{9,8},{10,9},{11,1... | collective-permute-start | bytes 6152 | tf_op jit(solution)/shard_map/ppermute | solution.py:19
  87.6 1.6 maximum_bitcast_fusion.1
  91.4 4.9 %pad_maximum_fusion = f32[3,3,512,512]{3,2,1,0:T(8,128)} fusion(f32[1,3,512,512]{3,2,1,0:T(8,128)S(1)} %maximum_bitcast_fusion.2, f32[1,3,512,512]{3,2,1,0:T(8,128)S(1)} %maximum_bitcast_fusion.1, f32[1,3,512,512]{3,2,1,0:T(8,128)S(1)} %maximum_bitcast_fusion), kind=kLoop, calls=%fused_computation | loop fusion | flops 4718592 | bytes 18874368 | tf_op jit(solution)/shard_map/stack | solution.py:73
  98.6 5.5 %collective-permute-start.19 = (bf16[1,8,512]{2,1,0:T(8,128)(2,1)S(1)}, bf16[1,8,512]{2,1,0:T(8,128)(2,1)S(1)}, u32[]{:S(2)}, u32[]{:S(2)}) collective-permute-start(bf16[1,8,512]{2,1,0:T(8,128)(2,1)S(1)} %get-tuple-element.91), channel_id=1, source_target_pairs={{0,16},{16,32},{32,48},{48,64},{64,80},{80,96},{96,112},{1,17},{17... | collective-permute-start | bytes 24584 | tf_op jit(solution)/shard_map/ppermute | solution.py:16
  107.6 1.3 convolution_add_fusion.29
  119.2 4.8 %collective-permute-start.9 = (bf16[16,1,128]{2,1,0:T(2,128)(2,1)S(1)}, bf16[16,1,128]{2,1,0:T(2,128)(2,1)S(1)}, u32[]{:S(2)}, u32[]{:S(2)}) collective-permute-start(bf16[16,1,128]{2,1,0:T(2,128)(2,1)S(1)} %get-tuple-element.67), channel_id=1, source_target_pairs={{1,0},{2,1},{3,2},{4,3},{5,4},{6,5},{7,6},{8,7},{9,8},{10,9},{11,1... | collective-permute-start | bytes 12296 | tf_op jit(solution)/shard_map/ppermute | solution.py:19
  125.9 5.4 %collective-permute-start.10 = (bf16[1,50,128]{2,1,0:T(8,128)(2,1)S(1)}, bf16[1,50,128]{2,1,0:T(8,128)(2,1)S(1)}, u32[]{:S(2)}, u32[]{:S(2)}) collective-permute-start(bf16[1,50,128]{2,1,0:T(8,128)(2,1)S(1)} %get-tuple-element.50), channel_id=1, source_target_pairs={{0,16},{16,32},{32,48},{48,64},{64,80},{80,96},{96,112},{1,17},{17... | collective-permute-start | bytes 38408 | tf_op jit(solution)/shard_map/ppermute | solution.py:16
  133.3 5.3 %collective-permute-done.11 = bf16[1,50,128]{2,1,0:T(8,128)(2,1)S(1)} collective-permute-done((bf16[1,50,128]{2,1,0:T(8,128)(2,1)S(1)}, bf16[1,50,128]{2,1,0:T(8,128)(2,1)S(1)}, u32[]{:S(2)}, u32[]{:S(2)}) %collective-permute-start.11) | collective-permute-done | bytes 12832 | tf_op jit(solution)/shard_map/ppermute | solution.py:19
  141.3 5.0 %collective-permute-start.21 = (bf16[16,1,128]{2,1,0:T(2,128)(2,1)S(1)}, bf16[16,1,128]{2,1,0:T(2,128)(2,1)S(1)}, u32[]{:S(2)}, u32[]{:S(2)}) collective-permute-start(bf16[16,1,128]{2,1,0:T(2,128)(2,1)S(1)} %get-tuple-element.59), channel_id=1, source_target_pairs={{1,0},{2,1},{3,2},{4,3},{5,4},{6,5},{7,6},{8,7},{9,8},{10,9},{11,1... | collective-permute-start | bytes 12296 | tf_op jit(solution)/shard_map/ppermute | solution.py:19
  148.4 6.9 %collective-permute-start.23 = (bf16[1,50,128]{2,1,0:T(8,128)(2,1)S(1)}, bf16[1,50,128]{2,1,0:T(8,128)(2,1)S(1)}, u32[]{:S(2)}, u32[]{:S(2)}) collective-permute-start(bf16[1,50,128]{2,1,0:T(8,128)(2,1)S(1)} %get-tuple-element.43), channel_id=1, source_target_pairs={{0,16},{16,32},{32,48},{48,64},{64,80},{80,96},{96,112},{1,17},{17... | collective-permute-start | bytes 38408 | tf_op jit(solution)/shard_map/ppermute | solution.py:16
  161.2 154.5 %all-reduce.3.cloned.1.call-done = (f32[3,3,128,128]{3,2,1,0:T(8,128)}, f32[128,512]{1,0:T(8,128)}, f32[3,3,512,512]{3,2,1,0:T(8,128)}, f32[512,128]{1,0:T(8,128)}, f32[3,3,128,128]{3,2,1,0:T(8,128)}) async-done(((f32[3,3,128,128]{3,2,1,0:T(8,128)}, f32[128,512]{1,0:T(8,128)}, f32[3,3,512,512]{3,2,1,0:T(8,128)}, f32[512,128]{1,0:T(8,128)}, f32[3,3,128,128]{3,2,1,0:T(8,128)}), (f32[3,3,128,128]{3,2,1,0:T(8,128)}, ...) | async-done | bytes 11141136 | tf_op jit(solution)/shard_map/psum | solution.py:132
  315.7 1.9 copy.23
  317.6 1.7 copy.24
  319.3 8.6 %copy.25 = f32[3,3,512,512]{3,2,1,0:T(8,128)} copy(f32[3,3,512,512]{3,2,1,0:T(8,128)} %get-tuple-element.112) | data formatting | bytes 18874368
  (256 shorter events, 73.5 us)
Async XLA Ops:
  7.2 308.5 %all-reduce.3.cloned.1.call-start = ((), (), s32[]{:S(2)}) async-start(), calls=%async_computation | async-start | bytes 22282240 | tf_op jit(solution)/shard_map/psum | solution.py:132
  8.1 15.3 %collective-permute-start.12 = (bf16[16,1,128]{2,1,0:T(2,128)(2,1)S(1)}, bf16[16,1,128]{2,1,0:T(2,128)(2,1)S(1)}, u32[]{:S(2)}, u32[]{:S(2)}) collective-permute-start(bf16[16,1,128]{2,1,0:T(2,128)(2,1)S(1)} %get-tuple-element.62), channel_id=1, source_target_pairs={{0,1},{1,2},{2,3},{3,4},{4,5},{5,6},{6,7},{7,8},{8,9},{9,10},{10,1... | collective-permute-start | bytes 12296 | tf_op jit(solution)/shard_map/ppermute | solution.py:16
  10.8 12.7 %collective-permute-start.13 = (bf16[16,1,128]{2,1,0:T(2,128)(2,1)S(1)}, bf16[16,1,128]{2,1,0:T(2,128)(2,1)S(1)}, u32[]{:S(2)}, u32[]{:S(2)}) collective-permute-start(bf16[16,1,128]{2,1,0:T(2,128)(2,1)S(1)} %get-tuple-element.63), channel_id=1, source_target_pairs={{1,0},{2,1},{3,2},{4,3},{5,4},{6,5},{7,6},{8,7},{9,8},{10,9},{11,1... | collective-permute-start | bytes 12296 | tf_op jit(solution)/shard_map/ppermute | solution.py:19
  11.6 5.1 %collective-permute-start = (bf16[16,1,128]{2,1,0:T(2,128)(2,1)S(1)}, bf16[16,1,128]{2,1,0:T(2,128)(2,1)S(1)}, u32[]{:S(2)}, u32[]{:S(2)}) collective-permute-start(bf16[16,1,128]{2,1,0:T(2,128)(2,1)S(1)} %get-tuple-element.70), channel_id=1, source_target_pairs={{0,1},{1,2},{2,3},{3,4},{4,5},{5,6},{6,7},{7,8},{8,9},{9,10},{10,1... | collective-permute-start | bytes 12296 | tf_op jit(solution)/shard_map/ppermute | solution.py:16
  17.4 16.8 %collective-permute-start.2 = (bf16[1,50,128]{2,1,0:T(8,128)(2,1)S(1)}, bf16[1,50,128]{2,1,0:T(8,128)(2,1)S(1)}, u32[]{:S(2)}, u32[]{:S(2)}) collective-permute-start(bf16[1,50,128]{2,1,0:T(8,128)(2,1)S(1)} %get-tuple-element.54), channel_id=1, source_target_pairs={{0,16},{16,32},{32,48},{48,64},{64,80},{80,96},{96,112},{1,17},{17... | collective-permute-start | bytes 38408 | tf_op jit(solution)/shard_map/ppermute | solution.py:16
  22.1 12.1 %collective-permute-start.3 = (bf16[1,50,128]{2,1,0:T(8,128)(2,1)S(1)}, bf16[1,50,128]{2,1,0:T(8,128)(2,1)S(1)}, u32[]{:S(2)}, u32[]{:S(2)}) collective-permute-start(bf16[1,50,128]{2,1,0:T(8,128)(2,1)S(1)} %get-tuple-element.55), channel_id=1, source_target_pairs={{16,0},{32,16},{48,32},{64,48},{80,64},{96,80},{112,96},{17,1},{33... | collective-permute-start | bytes 38408 | tf_op jit(solution)/shard_map/ppermute | solution.py:19
  24.2 13.5 %collective-permute-start.14 = (bf16[1,50,128]{2,1,0:T(8,128)(2,1)S(1)}, bf16[1,50,128]{2,1,0:T(8,128)(2,1)S(1)}, u32[]{:S(2)}, u32[]{:S(2)}) collective-permute-start(bf16[1,50,128]{2,1,0:T(8,128)(2,1)S(1)} %get-tuple-element.46), channel_id=1, source_target_pairs={{16,0},{32,16},{48,32},{64,48},{80,64},{96,80},{112,96},{17,1},{33... | collective-permute-start | bytes 38408 | tf_op jit(solution)/shard_map/ppermute | solution.py:19
  25.5 12.2 %collective-permute-start.15 = (bf16[1,50,128]{2,1,0:T(8,128)(2,1)S(1)}, bf16[1,50,128]{2,1,0:T(8,128)(2,1)S(1)}, u32[]{:S(2)}, u32[]{:S(2)}) collective-permute-start(bf16[1,50,128]{2,1,0:T(8,128)(2,1)S(1)} %get-tuple-element.47), channel_id=1, source_target_pairs={{0,16},{16,32},{32,48},{48,64},{64,80},{80,96},{96,112},{1,17},{17... | collective-permute-start | bytes 38408 | tf_op jit(solution)/shard_map/ppermute | solution.py:16
  38.6 7.3 %collective-permute-start.4 = (bf16[2,1,512]{2,1,0:T(2,128)(2,1)S(1)}, bf16[2,1,512]{2,1,0:T(2,128)(2,1)S(1)}, u32[]{:S(2)}, u32[]{:S(2)}) collective-permute-start(bf16[2,1,512]{2,1,0:T(2,128)(2,1)S(1)} %get-tuple-element.98), channel_id=1, source_target_pairs={{0,1},{1,2},{2,3},{3,4},{4,5},{5,6},{6,7},{7,8},{8,9},{9,10},{10,1... | collective-permute-start | bytes 6152 | tf_op jit(solution)/shard_map/ppermute | solution.py:16
  39.2 6.7 %collective-permute-start.5 = (bf16[2,1,512]{2,1,0:T(2,128)(2,1)S(1)}, bf16[2,1,512]{2,1,0:T(2,128)(2,1)S(1)}, u32[]{:S(2)}, u32[]{:S(2)}) collective-permute-start(bf16[2,1,512]{2,1,0:T(2,128)(2,1)S(1)} %get-tuple-element.99), channel_id=1, source_target_pairs={{1,0},{2,1},{3,2},{4,3},{5,4},{6,5},{7,6},{8,7},{9,8},{10,9},{11,1... | collective-permute-start | bytes 6152 | tf_op jit(solution)/shard_map/ppermute | solution.py:19
  46.0 7.4 %collective-permute-start.6 = (bf16[1,8,512]{2,1,0:T(8,128)(2,1)S(1)}, bf16[1,8,512]{2,1,0:T(8,128)(2,1)S(1)}, u32[]{:S(2)}, u32[]{:S(2)}) collective-permute-start(bf16[1,8,512]{2,1,0:T(8,128)(2,1)S(1)} %get-tuple-element.96), channel_id=1, source_target_pairs={{0,16},{16,32},{32,48},{48,64},{64,80},{80,96},{96,112},{1,17},{17... | collective-permute-start | bytes 24584 | tf_op jit(solution)/shard_map/ppermute | solution.py:16
  52.0 5.9 %collective-permute-start.7 = (bf16[1,8,512]{2,1,0:T(8,128)(2,1)S(1)}, bf16[1,8,512]{2,1,0:T(8,128)(2,1)S(1)}, u32[]{:S(2)}, u32[]{:S(2)}) collective-permute-start(bf16[1,8,512]{2,1,0:T(8,128)(2,1)S(1)} %get-tuple-element.97), channel_id=1, source_target_pairs={{16,0},{32,16},{48,32},{64,48},{80,64},{96,80},{112,96},{17,1},{33... | collective-permute-start | bytes 24584 | tf_op jit(solution)/shard_map/ppermute | solution.py:19
  80.9 16.4 %collective-permute-start.16 = (bf16[2,1,512]{2,1,0:T(2,128)(2,1)}, bf16[2,1,512]{2,1,0:T(2,128)(2,1)S(1)}, u32[]{:S(2)}, u32[]{:S(2)}) collective-permute-start(bf16[2,1,512]{2,1,0:T(2,128)(2,1)} %get-tuple-element.92), channel_id=1, source_target_pairs={{0,1},{1,2},{2,3},{3,4},{4,5},{5,6},{6,7},{7,8},{8,9},{9,10},{10,1... | collective-permute-start | bytes 6152 | tf_op jit(solution)/shard_map/ppermute | solution.py:16
  80.9 16.4 %collective-permute-start.17 = (bf16[2,1,512]{2,1,0:T(2,128)(2,1)}, bf16[2,1,512]{2,1,0:T(2,128)(2,1)S(1)}, u32[]{:S(2)}, u32[]{:S(2)}) collective-permute-start(bf16[2,1,512]{2,1,0:T(2,128)(2,1)} %get-tuple-element.93), channel_id=1, source_target_pairs={{1,0},{2,1},{3,2},{4,3},{5,4},{6,5},{7,6},{8,7},{9,8},{10,9},{11,1... | collective-permute-start | bytes 6152 | tf_op jit(solution)/shard_map/ppermute | solution.py:19
  97.3 6.9 %collective-permute-start.18 = (bf16[1,8,512]{2,1,0:T(8,128)(2,1)S(1)}, bf16[1,8,512]{2,1,0:T(8,128)(2,1)S(1)}, u32[]{:S(2)}, u32[]{:S(2)}) collective-permute-start(bf16[1,8,512]{2,1,0:T(8,128)(2,1)S(1)} %get-tuple-element.90), channel_id=1, source_target_pairs={{16,0},{32,16},{48,32},{64,48},{80,64},{96,80},{112,96},{17,1},{33... | collective-permute-start | bytes 24584 | tf_op jit(solution)/shard_map/ppermute | solution.py:19
  98.6 6.3 %collective-permute-start.19 = (bf16[1,8,512]{2,1,0:T(8,128)(2,1)S(1)}, bf16[1,8,512]{2,1,0:T(8,128)(2,1)S(1)}, u32[]{:S(2)}, u32[]{:S(2)}) collective-permute-start(bf16[1,8,512]{2,1,0:T(8,128)(2,1)S(1)} %get-tuple-element.91), channel_id=1, source_target_pairs={{0,16},{16,32},{32,48},{48,64},{64,80},{80,96},{96,112},{1,17},{17... | collective-permute-start | bytes 24584 | tf_op jit(solution)/shard_map/ppermute | solution.py:16
  119.1 6.8 %collective-permute-start.8 = (bf16[16,1,128]{2,1,0:T(2,128)(2,1)S(1)}, bf16[16,1,128]{2,1,0:T(2,128)(2,1)S(1)}, u32[]{:S(2)}, u32[]{:S(2)}) collective-permute-start(bf16[16,1,128]{2,1,0:T(2,128)(2,1)S(1)} %get-tuple-element.66), channel_id=1, source_target_pairs={{0,1},{1,2},{2,3},{3,4},{4,5},{5,6},{6,7},{7,8},{8,9},{9,10},{10,1... | collective-permute-start | bytes 12296 | tf_op jit(solution)/shard_map/ppermute | solution.py:16
  119.2 6.7 %collective-permute-start.9 = (bf16[16,1,128]{2,1,0:T(2,128)(2,1)S(1)}, bf16[16,1,128]{2,1,0:T(2,128)(2,1)S(1)}, u32[]{:S(2)}, u32[]{:S(2)}) collective-permute-start(bf16[16,1,128]{2,1,0:T(2,128)(2,1)S(1)} %get-tuple-element.67), channel_id=1, source_target_pairs={{1,0},{2,1},{3,2},{4,3},{5,4},{6,5},{7,6},{8,7},{9,8},{10,9},{11,1... | collective-permute-start | bytes 12296 | tf_op jit(solution)/shard_map/ppermute | solution.py:19
  125.9 7.4 %collective-permute-start.10 = (bf16[1,50,128]{2,1,0:T(8,128)(2,1)S(1)}, bf16[1,50,128]{2,1,0:T(8,128)(2,1)S(1)}, u32[]{:S(2)}, u32[]{:S(2)}) collective-permute-start(bf16[1,50,128]{2,1,0:T(8,128)(2,1)S(1)} %get-tuple-element.50), channel_id=1, source_target_pairs={{0,16},{16,32},{32,48},{48,64},{64,80},{80,96},{96,112},{1,17},{17... | collective-permute-start | bytes 38408 | tf_op jit(solution)/shard_map/ppermute | solution.py:16
  131.3 7.3 %collective-permute-start.11 = (bf16[1,50,128]{2,1,0:T(8,128)(2,1)S(1)}, bf16[1,50,128]{2,1,0:T(8,128)(2,1)S(1)}, u32[]{:S(2)}, u32[]{:S(2)}) collective-permute-start(bf16[1,50,128]{2,1,0:T(8,128)(2,1)S(1)} %get-tuple-element.51), channel_id=1, source_target_pairs={{16,0},{32,16},{48,32},{64,48},{80,64},{96,80},{112,96},{17,1},{33... | collective-permute-start | bytes 38408 | tf_op jit(solution)/shard_map/ppermute | solution.py:19
  141.2 5.7 %collective-permute-start.20 = (bf16[16,1,128]{2,1,0:T(2,128)(2,1)S(1)}, bf16[16,1,128]{2,1,0:T(2,128)(2,1)S(1)}, u32[]{:S(2)}, u32[]{:S(2)}) collective-permute-start(bf16[16,1,128]{2,1,0:T(2,128)(2,1)S(1)} %get-tuple-element.58), channel_id=1, source_target_pairs={{0,1},{1,2},{2,3},{3,4},{4,5},{5,6},{6,7},{7,8},{8,9},{9,10},{10,1... | collective-permute-start | bytes 12296 | tf_op jit(solution)/shard_map/ppermute | solution.py:16
  141.3 5.8 %collective-permute-start.21 = (bf16[16,1,128]{2,1,0:T(2,128)(2,1)S(1)}, bf16[16,1,128]{2,1,0:T(2,128)(2,1)S(1)}, u32[]{:S(2)}, u32[]{:S(2)}) collective-permute-start(bf16[16,1,128]{2,1,0:T(2,128)(2,1)S(1)} %get-tuple-element.59), channel_id=1, source_target_pairs={{1,0},{2,1},{3,2},{4,3},{5,4},{6,5},{7,6},{8,7},{9,8},{10,9},{11,1... | collective-permute-start | bytes 12296 | tf_op jit(solution)/shard_map/ppermute | solution.py:19
  147.1 8.3 %collective-permute-start.22 = (bf16[1,50,128]{2,1,0:T(8,128)(2,1)S(1)}, bf16[1,50,128]{2,1,0:T(8,128)(2,1)S(1)}, u32[]{:S(2)}, u32[]{:S(2)}) collective-permute-start(bf16[1,50,128]{2,1,0:T(8,128)(2,1)S(1)} %get-tuple-element.42), channel_id=1, source_target_pairs={{16,0},{32,16},{48,32},{64,48},{80,64},{96,80},{112,96},{17,1},{33... | collective-permute-start | bytes 38408 | tf_op jit(solution)/shard_map/ppermute | solution.py:19
  148.4 7.5 %collective-permute-start.23 = (bf16[1,50,128]{2,1,0:T(8,128)(2,1)S(1)}, bf16[1,50,128]{2,1,0:T(8,128)(2,1)S(1)}, u32[]{:S(2)}, u32[]{:S(2)}) collective-permute-start(bf16[1,50,128]{2,1,0:T(8,128)(2,1)S(1)} %get-tuple-element.43), channel_id=1, source_target_pairs={{0,16},{16,32},{32,48},{48,64},{64,80},{80,96},{96,112},{1,17},{17... | collective-permute-start | bytes 38408 | tf_op jit(solution)/shard_map/ppermute | solution.py:16
  (32 other events, 297.6 us)
Sparse Core Ops, SparseCore 0:
  141.3 174.3 all-reduce.2
where the time goes:
time: 338 us; the launch traced here: 336 us
  waiting for transfers between devices  166 us (49%)
  starting transfers between devices  68.2 us (20%)
  matrix products  50.7 us (15%)
  local copies, waits for them, and re-layouts  20.3 us (6%)
  other arithmetic  15.5 us (5%)
  between operations  15.4 us (5%)
    psum x1, waiting for transfers between devices, body(): lax.psum((g_enc, g_down, g_bot, g_up, g_dec), ('lat', 'lon'))  154 us
    ppermute x12, starting transfers between devices, padded(): lax.ppermute(lax.slice_in_dim(block, block.shape[dim] - width, None, axis...  40 us
    ppermute x12, starting transfers between devices, padded(): lax.ppermute(lax.slice_in_dim(block, 0, width, axis=dim), axis, backward)  28.1 us
    dot_general x27, matrix products, conv_back(): jnp.dot(view, kernel[tap_a, tap_b].T, preferred_element_type=jnp.float32)  17 us
    dot_general x27, matrix products, conv_fwd(): jnp.dot(view, kernel[tap_a, tap_b], preferred_element_type=jnp.float32)  16.7 us
    dot_general x29, matrix products, cross(): lax.dot_general(left.reshape(-1, left.shape[-1]), right.reshape(-1, right...  16.5 us
    unnamed x67, local copies, waits for them, and re-layouts  15.4 us
    ppermute x12, waiting for transfers between devices, padded(): lax.ppermute(lax.slice_in_dim(block, 0, width, axis=dim), axis, backward)  10.1 us
  transfers between devices with their start and end apart: 25, of which 7 were waited for; matrix products, arithmetic and copies ran while one was open for 9% of the time, Pallas kernels for 0%

commit v1 on v0

v1 whole, which is shorter than its diff:
```python
import jax
import jax.numpy as jnp
from jax import lax
from jax.experimental import pallas as pl
from jax.experimental.pallas import tpu as pltpu
from jax.sharding import PartitionSpec as P

POOL = 8
AXES = ("lat", "lon")
ROWS, COLS, DEPTH = 16, 48, 128
WIDE = 512
STRIDE = 64
EXT = 21 * STRIDE
RIM = 19 * STRIDE
OWN = ROWS * STRIDE
CROW, CCOL = ROWS // POOL, COLS // POOL
NLAT, NLON = 8, 16
COUNT = NLAT * NLON
GROW, GCOL = NLAT * CROW, NLON * CCOL
CELLS = GROW * GCOL
PACK = 2 * CROW * CCOL
WIN = 16
F32 = jnp.float32
BF16 = jnp.bfloat16


def mm(left, right, contract=((1,), (0,))):
    return lax.dot_general(left, right, (contract, ((), ())), preferred_element_type=F32)


def side_by_side(flat):
    wide = flat.astype(F32)
    low = pltpu.roll(wide, 1, 0).astype(BF16)
    high = pltpu.roll(wide, flat.shape[0] - 1, 0).astype(BF16)
    return jnp.concatenate([low, flat.astype(BF16), high], axis=1)


def split_two(value):
    high = value.astype(BF16)
    return high, (value - high.astype(F32)).astype(BF16)


def rim_position(shape, dim):
    spot = lax.broadcasted_iota(jnp.int32, shape, dim)
    slot = spot & (STRIDE - 1)
    line = spot >> 6
    left = slot == STRIDE - 1
    row = jnp.where(left, line - 1, line - 2)
    col = jnp.where(left, -1, slot)
    return row, col


def row_live(row, lat):
    return jnp.logical_and(
        jnp.logical_or(row >= 0, lat > 0), jnp.logical_or(row < ROWS, lat < NLAT - 1)
    )


def first_kernel(
    pos, fine, grad, top, bot, strip, w_enc, w_dec_t,
    pack, hid_out, slope_out, dm_out, fine_cat, own_grad, field, grad_cat,
):
    lat = pos[0]
    for part, (tile, cat) in enumerate(((fine, fine_cat), (grad, grad_cat))):
        lanes = slice(part * DEPTH, (part + 1) * DEPTH)
        field[0:1, 0:COLS, :] = jnp.zeros((1, COLS, DEPTH), BF16)
        field[1:3, 0:COLS, :] = top[:, :, lanes]
        field[3:19, 0:COLS, :] = tile[...]
        field[19:21, 0:COLS, :] = bot[:, :, lanes]
        field[:, COLS:STRIDE, :] = strip[:, :, lanes]
        cat[...] = side_by_side(field[...].reshape(EXT, DEPTH))
    act = jnp.zeros((RIM, DEPTH), F32)
    dm = jnp.zeros((RIM, DEPTH), F32)
    for tap in range(3):
        act = act + mm(fine_cat[tap * STRIDE : tap * STRIDE + RIM, :], w_enc[tap])
        dm = dm + mm(grad_cat[tap * STRIDE : tap * STRIDE + RIM, :], w_dec_t[tap])
    row, _ = rim_position((RIM, 1), 0)
    live = row_live(row, lat)
    sig = jax.nn.sigmoid(act)
    hid = jnp.where(live, act * sig, 0.0).astype(BF16)
    slope_out[...] = jnp.where(live, sig * (1.0 + act * (1.0 - sig)), 0.0)
    hid_out[...] = hid
    dm_out[...] = dm
    half = PACK // 2
    prow, pcol = rim_position((PACK, RIM), 1)
    which = lax.broadcasted_iota(jnp.int32, (PACK, RIM), 0)
    inside = (prow >= 0) & (prow < ROWS) & (pcol >= 0) & (pcol < COLS)
    cell = jnp.where(inside, (prow >> 3) * CCOL + (pcol >> 3), -1)
    take_hid = (cell == which).astype(F32).astype(BF16)
    take_dm = (inside & (cell + half == which)).astype(F32).astype(BF16)
    dm_high, dm_low = split_two(dm)
    packed = mm(take_hid, hid) * (1.0 / (POOL * POOL)) + (mm(take_dm, dm_high) + mm(take_dm, dm_low))
    packed = packed.astype(BF16)
    for peer in range(COUNT):
        pack[peer] = packed
    slot = lax.broadcasted_iota(jnp.int32, (OWN, 1), 0) & (STRIDE - 1)
    center = grad_cat[3 * STRIDE : 3 * STRIDE + OWN, DEPTH : 2 * DEPTH]
    own_grad[...] = jnp.where(slot < COLS, center, jnp.zeros_like(center))


def weight_kernel(w_down, w_bot, out):
    out[0] = mm(w_down[...], w_bot[0]).astype(BF16)


def third(value):
    return (value * 43) >> 8


def source_of(row, col, shift):
    inside = (row >= 0) & (row < GROW)
    col = jnp.where(col < 0, col + GCOL, col)
    col = jnp.where(col >= GCOL, col - GCOL, col)
    group = third(col)
    device = (row >> 1) * NLON + group
    return jnp.where(inside, device * PACK + shift + (row & 1) * CCOL + (col - group * CCOL), -1)


def second_kernel(
    pos, every, w_eff, w_up, hid, slope, dm, fine_cat, own_grad, parts, merged_cat, dact_cat
):
    lat, lon = pos[0], pos[1]
    spot = lax.broadcasted_iota(jnp.int32, (8 * WIN, 1), 0)
    line, slot = spot >> 4, spot & (WIN - 1)
    src = source_of(CROW * lat + line - 3, CCOL * lon + slot - 3, 0)
    src = jnp.where(slot < CCOL + 6, src, -1)
    spot = lax.broadcasted_iota(jnp.int32, (6 * WIN, 1), 0)
    line, slot = spot >> 4, spot & (WIN - 1)
    dsrc = source_of(CROW * lat + line - 2, CCOL * lon + slot - 2, CROW * CCOL)
    dsrc = jnp.where(slot < CCOL + 4, dsrc, -1)
    spots = lax.broadcasted_iota(jnp.int32, (8 * WIN, COUNT * PACK), 1)
    pooled = mm((spots == src).astype(F32).astype(BF16), every[...])
    spots = lax.broadcasted_iota(jnp.int32, (6 * WIN, COUNT * PACK), 1)
    dlift = mm((spots == dsrc).astype(F32).astype(BF16), every[...]).astype(BF16)
    shifted = [pooled.astype(BF16)] + [
        pltpu.roll(pooled, 8 * WIN - step, 0).astype(BF16) for step in (1, 2)
    ]
    pooled_cat = jnp.concatenate(shifted, axis=1)
    zpre = jnp.zeros((6 * WIN, WIDE), F32)
    for tap in range(3):
        zpre = zpre + mm(
            pooled_cat[tap * WIN : tap * WIN + 6 * WIN], w_eff[tap * 384 : tap * 384 + 384, :]
        )
    sig = jax.nn.sigmoid(zpre)
    zact = (zpre * sig).astype(BF16)
    dz = mm(dlift, w_up[...], ((1,), (1,))) * (sig * (1.0 + zpre * (1.0 - sig)))
    dz = dz.astype(BF16).astype(F32)
    lifted = mm(zact, w_up[...])
    gap = jnp.zeros((WIN, WIDE), F32)
    padded = jnp.concatenate([gap, dz, gap], axis=0)
    dpool = jnp.zeros((6 * WIN, DEPTH), F32)
    for tap_b in range(3):
        turn = (1 - tap_b) % (8 * WIN)
        moved = (padded if turn == 0 else pltpu.roll(padded, turn, 0)).astype(BF16)
        for tap_a in range(3):
            spot = ((2 - tap_a) * 3 + (2 - tap_b)) * DEPTH
            dpool = dpool + mm(
                moved[tap_a * WIN : tap_a * WIN + 6 * WIN],
                w_eff[spot : spot + DEPTH, :],
                ((1,), (1,)),
            )
    dpool = dpool * (1.0 / (POOL * POOL))
    lift_high, lift_low = split_two(lifted)
    pool_high, pool_low = split_two(dpool)
    tail = jnp.zeros((2 * WIN, 2 * DEPTH), BF16)
    table = jnp.concatenate(
        [
            jnp.concatenate([lift_high, pool_high], axis=1),
            tail,
            jnp.concatenate([lift_low, pool_low], axis=1),
            tail,
        ],
        axis=0,
    )
    row, col = rim_position((RIM, 1), 0)
    home = (((row + POOL) >> 3) + 1) * WIN + ((col + POOL) >> 3) + 1
    home = jnp.where(col <= COLS, home, -1)
    cells = lax.broadcasted_iota(jnp.int32, (RIM, 256), 1) & 127
    spread = mm((cells == home).astype(F32).astype(BF16), table)
    live = row_live(row, lat)
    merged = jnp.where(live, hid[...].astype(F32) + spread[:, :DEPTH], 0.0)
    dact = (dm[...] + spread[:, DEPTH:]) * slope[...]
    merged_cat[...] = side_by_side(merged.astype(BF16))
    dact_cat[...] = side_by_side(dact.astype(BF16))
    slot = lax.broadcasted_iota(jnp.int32, (OWN, 1), 0) & (STRIDE - 1)
    center = dact_cat[2 * STRIDE : 2 * STRIDE + OWN, DEPTH : 2 * DEPTH]
    own_dact = jnp.where(slot < COLS, center, jnp.zeros_like(center))
    for tap in range(3):
        start = (tap + 1) * STRIDE
        parts[tap * 384 : tap * 384 + 384, :] = mm(
            merged_cat[start : start + OWN, :], own_grad[...], ((0,), (0,))
        ).astype(BF16)
        start = (tap + 2) * STRIDE
        parts[1152 + tap * 384 : 1152 + tap * 384 + 384, :] = mm(
            fine_cat[start : start + OWN, :], own_dact, ((0,), (0,))
        ).astype(BF16)
    parts[2304:, :] = jnp.zeros((COUNT * PACK - 2304, DEPTH), BF16)


def third_kernel(merged_cat, dact_cat, w_dec, w_enc_t, block_out, field_grad):
    out = jnp.zeros((OWN, DEPTH), F32)
    back = jnp.zeros((OWN, DEPTH), F32)
    for tap in range(3):
        start = (tap + 1) * STRIDE
        out = out + mm(merged_cat[start : start + OWN, :], w_dec[tap])
        back = back + mm(dact_cat[start : start + OWN, :], w_enc_t[tap])
    block_out[...] = out.astype(BF16).reshape(ROWS, STRIDE, DEPTH)[:, :COLS, :]
    field_grad[...] = back.astype(BF16).reshape(ROWS, STRIDE, DEPTH)[:, :COLS, :]


def coarse_kernel(
    every, w_eff, w_up, w_down, w_bot, g_bot, g_down, g_up, pooled_cat, dlift, zact, dz, table
):
    step = pl.program_id(0)
    line = 2 * GCOL

    @pl.when(step == 0)
    def _():
        block = NLON * PACK
        spot = lax.broadcasted_iota(jnp.int32, (4 * line, 1), 0)
        kind = (spot >= line).astype(jnp.int32) + (spot >= 2 * line).astype(jnp.int32)
        kind = kind + (spot >= 3 * line).astype(jnp.int32)
        within = spot - kind * line
        row = (within >= GCOL).astype(jnp.int32)
        col = within - row * GCOL
        col = jnp.where(kind < 3, col + kind - 1, col)
        shift = jnp.where(kind < 3, 0, CROW * CCOL)
        src = source_of(row, col, shift)
        spots = lax.broadcasted_iota(jnp.int32, (4 * line, block), 1)
        order = (spots == src).astype(F32).astype(BF16)
        edge = jnp.zeros((GCOL, 3 * DEPTH), BF16)
        pooled_cat[0:GCOL, :] = edge
        pooled_cat[(GROW + 1) * GCOL :, :] = edge
        for pair in range(NLAT // 2):
            both = jnp.concatenate(
                [every[(2 * pair + k) * block : (2 * pair + k + 1) * block, :] for k in (0, 1)],
                axis=1,
            )
            moved = mm(order, both).astype(BF16)
            for k in (0, 1):
                lat = 2 * pair + k
                lanes = slice(k * DEPTH, (k + 1) * DEPTH)
                at = GCOL + lat * line
                for b in range(3):
                    pooled_cat[at : at + line, b * DEPTH : (b + 1) * DEPTH] = moved[
                        b * line : (b + 1) * line, lanes
                    ]
                dlift[lat * line : (lat + 1) * line, :] = moved[3 * line :, lanes]
        for part in range(NLAT):
            base = part * line
            zpre = jnp.zeros((line, WIDE), F32)
            for tap in range(3):
                at = base + tap * GCOL
                zpre = zpre + mm(pooled_cat[at : at + line, :], w_eff[tap * 384 : tap * 384 + 384, :])
            sig = jax.nn.sigmoid(zpre)
            zact[base : base + line, :] = (zpre * sig).astype(BF16)
            up = mm(dlift[base : base + line, :], w_up[...], ((1,), (1,)))
            dz[base : base + line, :] = (up * (sig * (1.0 + zpre * (1.0 - sig)))).astype(BF16)
        g_up[...] = mm(zact[...], dlift[...], ((0,), (0,)))
        g_down[...] = jnp.zeros((DEPTH, WIDE), F32)
        for tap in range(3):
            at = tap * GCOL
            corr = mm(pooled_cat[at : at + CELLS, :], dz[...], ((0,), (0,)))
            high, low = split_two(corr)
            for b in range(3):
                lanes = slice(b * DEPTH, (b + 1) * DEPTH)
                table[tap * 3 + b, 0:DEPTH, :] = high[lanes]
                table[tap * 3 + b, DEPTH:, :] = low[lanes]

    pair = table[step]
    twice = jnp.concatenate([w_down[...], w_down[...]], axis=0)
    g_bot[0] = mm(twice, pair, ((0,), (0,)))
    back = mm(pair, w_bot[0], ((1,), (1,)))
    g_down[...] += back[:DEPTH] + back[DEPTH:]


def vmem():
    return pl.BlockSpec(memory_space=pltpu.VMEM)


def smem():
    return pl.BlockSpec(memory_space=pltpu.SMEM)


def shape(dims, kind):
    return jax.ShapeDtypeStruct(dims, kind)


PARAMS = dict(compiler_params=pltpu.CompilerParams(vmem_limit_bytes=56 * 1024 * 1024))


def turned(kernel):
    flipped = jnp.flip(kernel, (0, 1)).swapaxes(2, 3)
    return flipped.reshape(3, 3 * kernel.shape[3], kernel.shape[2])


def body(fine, w_enc, w_down, w_bot, w_up, w_dec, grad):
    pos = jnp.stack([lax.axis_index("lat"), lax.axis_index("lon")]).astype(jnp.int32)
    down = [(i, i + 1) for i in range(NLAT - 1)]
    up = [(t, s) for s, t in down]
    right = [(i, (i + 1) % NLON) for i in range(NLON)]
    left = [(t, s) for s, t in right]
    both = jnp.concatenate([fine, grad], axis=2)
    top = lax.ppermute(both[-2:], "lat", down)
    bot = lax.ppermute(both[:2], "lat", up)
    first = jnp.concatenate([top[:, :2], both[:, :2], bot[:, :2]], axis=0)
    last = jnp.concatenate([top[:, -2:], both[:, -2:], bot[:, -2:]], axis=0)
    low = lax.ppermute(last, "lon", right)
    high = lax.ppermute(first, "lon", left)
    strip = jnp.concatenate(
        [
            jnp.pad(high, ((1, 0), (0, 0), (0, 0))),
            jnp.zeros((21, 12, 2 * DEPTH), BF16),
            jnp.pad(low, ((0, 1), (0, 0), (0, 0))),
        ],
        axis=1,
    )
    w_eff = pl.pallas_call(
        weight_kernel,
        grid=(9,),
        in_specs=[
            pl.BlockSpec((DEPTH, WIDE), lambda i: (0, 0)),
            pl.BlockSpec((1, WIDE, WIDE), lambda i: (i, 0, 0)),
        ],
        out_specs=pl.BlockSpec((1, DEPTH, WIDE), lambda i: (i, 0, 0)),
        out_shape=shape((9, DEPTH, WIDE), BF16),
        name="weights",
    )(w_down, w_bot.reshape(9, WIDE, WIDE)).reshape(9 * DEPTH, WIDE)
    w_enc_f = w_enc.reshape(3, 3 * DEPTH, DEPTH)
    w_dec_f = w_dec.reshape(3, 3 * DEPTH, DEPTH)
    pack, hid, slope, dm, fine_cat, own_grad = pl.pallas_call(
        first_kernel,
        in_specs=[smem()] + [vmem()] * 7,
        out_specs=[vmem()] * 6,
        out_shape=[
            shape((COUNT, PACK, DEPTH), BF16),
            shape((RIM, DEPTH), BF16),
            shape((RIM, DEPTH), F32),
            shape((RIM, DEPTH), F32),
            shape((EXT, 3 * DEPTH), BF16),
            shape((OWN, DEPTH), BF16),
        ],
        scratch_shapes=[
            pltpu.VMEM((21, STRIDE, DEPTH), BF16),
            pltpu.VMEM((EXT, 3 * DEPTH), BF16),
        ],
        name="first",
        **PARAMS,
    )(pos, fine, grad, top, bot, strip, w_enc_f, turned(w_dec))
    every = lax.all_to_all(pack, AXES, 0, 0).reshape(COUNT * PACK, DEPTH)
    parts, merged_cat, dact_cat = pl.pallas_call(
        second_kernel,
        in_specs=[smem()] + [vmem()] * 8,
        out_specs=[vmem()] * 3,
        out_shape=[
            shape((COUNT * PACK, DEPTH), BF16),
            shape((RIM, 3 * DEPTH), BF16),
            shape((RIM, 3 * DEPTH), BF16),
        ],
        name="second",
        **PARAMS,
    )(pos, every, w_eff, w_up, hid, slope, dm, fine_cat, own_grad)
    spread = lax.all_to_all(parts.reshape(COUNT, PACK, DEPTH), AXES, 0, 0)
    total = spread.astype(F32).sum(axis=0).astype(BF16)
    whole = lax.all_to_all(jnp.broadcast_to(total[None], (COUNT, PACK, DEPTH)), AXES, 0, 0)
    whole = whole.reshape(COUNT * PACK, DEPTH)
    g_dec = whole[:1152].astype(F32).reshape(3, 3, DEPTH, DEPTH)
    g_enc = whole[1152:2304].astype(F32).reshape(3, 3, DEPTH, DEPTH)
    block_out, field_grad = pl.pallas_call(
        third_kernel,
        in_specs=[vmem()] * 4,
        out_specs=[vmem()] * 2,
        out_shape=[shape((ROWS, COLS, DEPTH), BF16)] * 2,
        name="third",
        **PARAMS,
    )(merged_cat, dact_cat, w_dec_f, turned(w_enc))
    g_bot, g_down, g_up = pl.pallas_call(
        coarse_kernel,
        grid=(9,),
        in_specs=[
            pl.BlockSpec((COUNT * PACK, DEPTH), lambda i: (0, 0)),
            pl.BlockSpec((9 * DEPTH, WIDE), lambda i: (0, 0)),
            pl.BlockSpec((WIDE, DEPTH), lambda i: (0, 0)),
            pl.BlockSpec((DEPTH, WIDE), lambda i: (0, 0)),
            pl.BlockSpec((1, WIDE, WIDE), lambda i: (i, 0, 0)),
        ],
        out_specs=[
            pl.BlockSpec((1, WIDE, WIDE), lambda i: (i, 0, 0)),
            pl.BlockSpec((DEPTH, WIDE), lambda i: (0, 0)),
            pl.BlockSpec((WIDE, DEPTH), lambda i: (0, 0)),
        ],
        out_shape=[
            shape((9, WIDE, WIDE), F32),
            shape((DEPTH, WIDE), F32),
            shape((WIDE, DEPTH), F32),
        ],
        scratch_shapes=[
            pltpu.VMEM(((GROW + 2) * GCOL, 3 * DEPTH), BF16),
            pltpu.VMEM((CELLS, DEPTH), BF16),
            pltpu.VMEM((CELLS, WIDE), BF16),
            pltpu.VMEM((CELLS, WIDE), BF16),
            pltpu.VMEM((9, 2 * DEPTH, WIDE), BF16),
        ],
        name="coarse",
        **PARAMS,
    )(every, w_eff, w_up, w_down, w_bot.reshape(9, WIDE, WIDE))
    return (block_out, field_grad, g_enc, g_down, g_bot.reshape(3, 3, WIDE, WIDE), g_up, g_dec)


def solution(mesh):
    return jax.shard_map(
        body,
        mesh=mesh,
        in_specs=(P("lat", "lon", None), P(), P(), P(), P(), P(), P("lat", "lon", None)),
        out_specs=(P("lat", "lon", None), P("lat", "lon", None), P(), P(), P(), P(), P()),
        check_vma=False,
    )
```

time: 338 us -> 112 us (0.33)
  waiting for transfers between devices: 166 us -> 15.3 us
  matrix products: 50.7 us -> 0 us
  starting transfers between devices: 68.2 us -> 23.9 us
  Pallas kernels: 0 us -> 39.9 us
  blocking collectives: 0 us -> 21.2 us
  between operations: 15.4 us -> 0.77 us
  local copies, waits for them, and re-layouts: 20.3 us -> 6.83 us
  other arithmetic: 15.5 us -> 3.31 us
    psum x1 -> x0, waiting for transfers between devices: 154 us -> none  [body(): lax.psum((g_enc, g_down, g_bot, g_up, g_dec), ('lat', 'lon'))]
    ppermute x24 -> x4, starting transfers between devices: 68.1 us -> 9.21 us  [the longest x1 5.47 us: body(): top = lax.ppermute(both[-2:], 'lat', down)]
    dot_general x87 -> x0, matrix products: 50.7 us -> none  [the longest x27 17 us: conv_back(): jnp.dot(view, kernel[tap_a, tap_b].T, preferred_element_type=jnp.float32)]
    pallas_call x0 -> x5, Pallas kernels: none -> 39.9 us  [the longest x1 16.6 us: body(): pl.pallas_call(coarse_kernel, grid=(9,), in_specs=[pl.BlockSpec((COUNT *...]
    all_to_all x0 -> x1, blocking collectives: none -> 21.2 us  [body(): spread = lax.all_to_all(parts.reshape(COUNT, PACK, DEPTH), AXES, 0, 0)]
    all_to_all x0 -> x2, starting transfers between devices: none -> 14.7 us  [the longest x1 10.5 us: body(): every = lax.all_to_all(pack, AXES, 0, 0).reshape(COUNT * PACK, DEPTH)]
    unnamed x67 -> x9, local copies, waits for them, and re-layouts: 15.4 us -> 1.88 us
    all_to_all x0 -> x2, waiting for transfers between devices: none -> 9.2 us  [the longest x1 9.2 us: body(): every = lax.all_to_all(pack, AXES, 0, 0).reshape(COUNT * PACK, DEPTH)]
  transfers between devices with their start and end apart: 25 -> 6, of which waited for: 7 -> 3; matrix products, arithmetic and copies ran while one was open for 9% -> 3% of each run, Pallas kernels for 0% -> 25%
where the time goes in v1:
time: 112 us; the launch traced here: 111 us
  Pallas kernels  39.9 us (36%)
  starting transfers between devices  23.9 us (21%)
  blocking collectives  21.2 us (19%)
  waiting for transfers between devices  15.3 us (14%)
  local copies, waits for them, and re-layouts  6.83 us (6%)
  other arithmetic  3.31 us (3%)
    all_to_all x1, blocking collectives, body(): spread = lax.all_to_all(parts.reshape(COUNT, PACK, DEPTH), AXES, 0, 0)  21.2 us
    pallas_call x1, Pallas kernels, body(): pl.pallas_call(coarse_kernel, grid=(9,), in_specs=[pl.BlockSpec((COUNT *...  16.6 us
    all_to_all x1, starting transfers between devices, body(): every = lax.all_to_all(pack, AXES, 0, 0).reshape(COUNT * PACK, DEPTH)  10.5 us
    all_to_all x1, waiting for transfers between devices, body(): every = lax.all_to_all(pack, AXES, 0, 0).reshape(COUNT * PACK, DEPTH)  9.2 us
    pallas_call x1, Pallas kernels, body(): pl.pallas_call(weight_kernel, grid=(9,), in_specs=[pl.BlockSpec((DEPTH, W...  7.41 us
    pallas_call x1, Pallas kernels, body(): pl.pallas_call(second_kernel, in_specs=[smem()] + [vmem()] * 8, out_specs...  7.12 us
    ppermute x1, starting transfers between devices, body(): top = lax.ppermute(both[-2:], 'lat', down)  5.47 us
    pallas_call x1, Pallas kernels, body(): pl.pallas_call(first_kernel, in_specs=[smem()] + [vmem()] * 7, out_specs=...  5.02 us
  transfers between devices with their start and end apart: 6, of which 3 were waited for; matrix products, arithmetic and copies ran while one was open for 3% of the time, Pallas kernels for 25%

profile of v1, /device:TPU:1, one launch (start us, length us, event | category | flops | bytes accessed | tf_op | source)
XLA Modules:
  0.0 111.2 jit_solution(15220448040876036951)
XLA Ops:
  0.6 1.0 constant_dynamic-update-slice_fusion.1
  1.6 1.0 constant_dynamic-update-slice_fusion
  2.6 5.5 %collective-permute-start = (bf16[2,48,256]{2,1,0:T(8,128)(2,1)S(1)}, bf16[2,48,256]{2,1,0:T(8,128)(2,1)S(1)}, u32[]{:S(2)}, u32[]{:S(2)}) collective-permute-start(bf16[2,48,256]{2,1,0:T(8,128)(2,1)S(1)} %get-tuple-element.40), channel_id=1, source_target_pairs={{0,16},{16,32},{32,48},{48,64},{64,80},{80,96},{96,112},{1,17},{17... | collective-permute-start | bytes 147464 | tf_op jit(solution)/shard_map/ppermute | solution.py:303
  8.1 1.3 %collective-permute-start.1 = (bf16[2,48,256]{2,1,0:T(8,128)(2,1)S(1)}, bf16[2,48,256]{2,1,0:T(8,128)(2,1)S(1)}, u32[]{:S(2)}, u32[]{:S(2)}) collective-permute-start(bf16[2,48,256]{2,1,0:T(8,128)(2,1)S(1)} %get-tuple-element.39), channel_id=1, source_target_pairs={{16,0},{32,16},{48,32},{64,48},{80,64},{96,80},{112,96},{17,1},{33... | collective-permute-start | bytes 147464 | tf_op jit(solution)/shard_map/ppermute | solution.py:304
  9.4 1.0 reverse_bitcast_fusion.1
  10.4 4.0 %collective-permute-done.1.bot = bf16[2,48,256]{2,1,0:T(8,128)(2,1)S(1)} collective-permute-done((bf16[2,48,256]{2,1,0:T(8,128)(2,1)S(1)}, bf16[2,48,256]{2,1,0:T(8,128)(2,1)S(1)}, u32[]{:S(2)}, u32[]{:S(2)}) %collective-permute-start.1) | collective-permute-done | bytes 49184 | tf_op jit(solution)/shard_map/ppermute | solution.py:304
  14.5 2.4 %collective-permute-start.3 = (bf16[20,2,256]{2,1,0:T(2,128)(2,1)S(1)}, bf16[20,2,256]{2,1,0:T(2,128)(2,1)S(1)}, u32[]{:S(2)}, u32[]{:S(2)}) collective-permute-start(bf16[20,2,256]{2,1,0:T(2,128)(2,1)S(1)} %pad_maximum_fusion.1), channel_id=1, source_target_pairs={{0,1},{1,2},{2,3},{3,4},{4,5},{5,6},{6,7},{7,8},{8,9},{9,10},{10,1... | collective-permute-start | bytes 61448 | tf_op jit(solution)/shard_map/ppermute | solution.py:307
  17.6 0.9 copy.14
  18.6 2.1 %collective-permute-done.2 = bf16[20,2,256]{2,1,0:T(2,128)(2,1)S(1)} collective-permute-done((bf16[20,2,256]{2,1,0:T(2,128)(2,1)S(1)}, bf16[20,2,256]{2,1,0:T(2,128)(2,1)S(1)}, u32[]{:S(2)}, u32[]{:S(2)}) %collective-permute-start.2) | collective-permute-done | bytes 20512 | tf_op jit(solution)/shard_map/ppermute | solution.py:308
  20.7 0.8 fusion.2.strip
  21.4 5.0 %first.1 = (bf16[128,24,128]{2,1,0:T(8,128)(2,1)}, bf16[1216,128]{1,0:T(8,128)(2,1)}, f32[1216,128]{1,0:T(8,128)}, f32[1216,128]{1,0:T(8,128)}, bf16[1344,384]{1,0:T(8,128)(2,1)}, /*index=5*/bf16[1024,128]{1,0:T(8,128)(2,1)}) custom-call(s32[2]{0:T(128)} %pad_add_fusion.pos, bf16[16,48,128]{2,1,0:T(8,128)(2,1)} %fine.1, bf16[16,48,128]{2,1,0:T(8,128)(2,1)} %grad.1, ...), custom_call_target="tpu_custom_call" | custom-call | tf_op jit(solution)/shard_map/first/pallas_call | solution.py:330
  26.5 10.5 %all-to-all-start = ((bf16[128,24,128]{2,1,0:T(8,128)(2,1)}), bf16[128,24,128]{2,1,0:T(8,128)(2,1)S(1)}, u32[]{:S(2)}, u32[]{:S(2)}) async-start(bf16[128,24,128]{2,1,0:T(8,128)(2,1)} %get-tuple-element.21), calls=%async_computation | async-start | bytes 1572864 | tf_op jit(solution)/shard_map/all_to_all | solution.py:349
  37.0 7.4 %weights.1 = bf16[9,128,512]{2,1,0:T(8,128)(2,1)} custom-call(bf16[128,512]{1,0:T(8,128)(2,1)} %w_down.3, bf16[9,512,512]{2,1,0:T(8,128)(2,1)} %bitcast.19), custom_call_target="tpu_custom_call" | custom-call | tf_op jit(solution)/shard_map/weights/pallas_call | solution.py:317
  44.4 9.2 %all-to-all-done = bf16[128,24,128]{2,1,0:T(8,128)(2,1)S(1)} async-done(((bf16[128,24,128]{2,1,0:T(8,128)(2,1)}), bf16[128,24,128]{2,1,0:T(8,128)(2,1)S(1)}, u32[]{:S(2)}, u32[]{:S(2)}) %all-to-all-start) | async-done | bytes 786464 | tf_op jit(solution)/shard_map/all_to_all | solution.py:349
  53.6 0.9 copy-done
  54.5 7.1 %second.1 = (bf16[3072,128]{1,0:T(8,128)(2,1)}, bf16[1216,384]{1,0:T(8,128)(2,1)}, bf16[1216,384]{1,0:T(8,128)(2,1)}) custom-call(s32[2]{0:T(128)} %pad_add_fusion.pos, bf16[3072,128]{1,0:T(8,128)(2,1)} %bitcast.23, bf16[1152,512]{1,0:T(8,128)(2,1)} %bitcast.21, bf16[512,128]{1,0:T(8,128)(2,1)} %w_up.3, bf16[1216,128]{1,0:T(8,128)(2,1)} %get-tuple-element.22.hid, ...), custom_call_target="tpu_custom_call" | custom-call | tf_op jit(solution)/shard_map/second/pallas_call | solution.py:350
  61.6 21.2 %all_to_all.15 = bf16[128,24,128]{2,1,0:T(8,128)(2,1)S(1)} all-to-all(bf16[128,24,128]{2,1,0:T(8,128)(2,1)} %bitcast.31), channel_id=1, replica_groups=mesh['lat'=8,'lon'=16] {'lat','lon'}, dimensions={0} | all-to-all | bytes 1572864 | tf_op jit(solution)/shard_map/all_to_all | solution.py:362
  82.9 1.0 broadcast_in_dim.10
  83.9 4.2 %all-to-all-start.2 = ((bf16[128,24,128]{2,1,0:T(8,128)(2,1)}), bf16[128,24,128]{2,1,0:T(8,128)(2,1)S(1)}, u32[]{:S(2)}, u32[]{:S(2)}) async-start(bf16[128,24,128]{2,1,0:T(8,128)(2,1)} %broadcast_in_dim.10), calls=%async_computation.2 | async-start | bytes 1572864 | tf_op jit(solution)/shard_map/all_to_all | solution.py:364
  88.2 0.9 copy.15
  89.0 16.6 %coarse.1 = (f32[9,512,512]{2,1,0:T(8,128)}, f32[128,512]{1,0:T(8,128)}, f32[512,128]{1,0:T(8,128)}) custom-call(bf16[3072,128]{1,0:T(8,128)(2,1)} %bitcast.24, bf16[1152,512]{1,0:T(8,128)(2,1)} %bitcast.22, bf16[512,128]{1,0:T(8,128)(2,1)} %w_up.3, bf16[128,512]{1,0:T(8,128)(2,1)} %w_down.3, bf16[9,512,512]{2,1,0:T(8,128)(2,1)} %bitcast.20), custom_call_target="tpu_custom_call" | custom-call | tf_op jit(solution)/shard_map/coarse/pallas_call | solution.py:376
  105.7 3.7 %third.1 = (bf16[16,48,128]{2,1,0:T(8,128)(2,1)}, bf16[16,48,128]{2,1,0:T(8,128)(2,1)}) custom-call(bf16[1216,384]{1,0:T(8,128)(2,1)} %get-tuple-element.27.merged_cat, bf16[1216,384]{1,0:T(8,128)(2,1)} %get-tuple-element.28.dact_cat, bf16[3,384,128]{2,1,0:T(8,128)(2,1)} %bitcast.25, bf16[3,384,128]{2,1,0:T(8,128)(2,1)} %bitcast.26), custom_call_target="tpu_custom_call" | custom-call | tf_op jit(solution)/shard_map/third/pallas_call | solution.py:368
  109.4 0.9 convert.3
  110.3 0.9 convert.4
  (23 shorter events, 1.1 us)
Async XLA Ops:
  2.6 11.8 %collective-permute-start = (bf16[2,48,256]{2,1,0:T(8,128)(2,1)S(1)}, bf16[2,48,256]{2,1,0:T(8,128)(2,1)S(1)}, u32[]{:S(2)}, u32[]{:S(2)}) collective-permute-start(bf16[2,48,256]{2,1,0:T(8,128)(2,1)S(1)} %get-tuple-element.40), channel_id=1, source_target_pairs={{0,16},{16,32},{32,48},{48,64},{64,80},{80,96},{96,112},{1,17},{17... | collective-permute-start | bytes 147464 | tf_op jit(solution)/shard_map/ppermute | solution.py:303
  8.1 6.3 %collective-permute-start.1 = (bf16[2,48,256]{2,1,0:T(8,128)(2,1)S(1)}, bf16[2,48,256]{2,1,0:T(8,128)(2,1)S(1)}, u32[]{:S(2)}, u32[]{:S(2)}) collective-permute-start(bf16[2,48,256]{2,1,0:T(8,128)(2,1)S(1)} %get-tuple-element.39), channel_id=1, source_target_pairs={{16,0},{32,16},{48,32},{64,48},{80,64},{96,80},{112,96},{17,1},{33... | collective-permute-start | bytes 147464 | tf_op jit(solution)/shard_map/ppermute | solution.py:304
  14.4 7.0 %copy-start.3 = (bf16[2,48,256]{2,1,0:T(8,128)(2,1)}, bf16[2,48,256]{2,1,0:T(8,128)(2,1)S(1)}, u32[]{:S(2)}) copy-start(bf16[2,48,256]{2,1,0:T(8,128)(2,1)S(1)} %collective-permute-done.1.bot) | copy-start | bytes 147460
  14.4 7.0 %copy-start.2 = (bf16[2,48,256]{2,1,0:T(8,128)(2,1)}, bf16[2,48,256]{2,1,0:T(8,128)(2,1)S(1)}, u32[]{:S(2)}) copy-start(bf16[2,48,256]{2,1,0:T(8,128)(2,1)S(1)} %collective-permute-done.top) | copy-start | bytes 147460
  14.5 4.1 %collective-permute-start.3 = (bf16[20,2,256]{2,1,0:T(2,128)(2,1)S(1)}, bf16[20,2,256]{2,1,0:T(2,128)(2,1)S(1)}, u32[]{:S(2)}, u32[]{:S(2)}) collective-permute-start(bf16[20,2,256]{2,1,0:T(2,128)(2,1)S(1)} %pad_maximum_fusion.1), channel_id=1, source_target_pairs={{0,1},{1,2},{2,3},{3,4},{4,5},{5,6},{6,7},{7,8},{8,9},{9,10},{10,1... | collective-permute-start | bytes 61448 | tf_op jit(solution)/shard_map/ppermute | solution.py:307
  16.9 3.8 %collective-permute-start.2 = (bf16[20,2,256]{2,1,0:T(2,128)(2,1)S(1)}, bf16[20,2,256]{2,1,0:T(2,128)(2,1)S(1)}, u32[]{:S(2)}, u32[]{:S(2)}) collective-permute-start(bf16[20,2,256]{2,1,0:T(2,128)(2,1)S(1)} %pad_maximum_fusion), channel_id=1, source_target_pairs={{1,0},{2,1},{3,2},{4,3},{5,4},{6,5},{7,6},{8,7},{9,8},{10,9},{11,1... | collective-permute-start | bytes 61448 | tf_op jit(solution)/shard_map/ppermute | solution.py:308
  26.5 27.1 %all-to-all-start = ((bf16[128,24,128]{2,1,0:T(8,128)(2,1)}), bf16[128,24,128]{2,1,0:T(8,128)(2,1)S(1)}, u32[]{:S(2)}, u32[]{:S(2)}) async-start(bf16[128,24,128]{2,1,0:T(8,128)(2,1)} %get-tuple-element.21), calls=%async_computation | async-start | bytes 1572864 | tf_op jit(solution)/shard_map/all_to_all | solution.py:349
  53.6 0.9 copy-start
  54.5 33.6 %copy-start.1 = (bf16[3,3,128,128]{3,2,1,0:T(8,128)(2,1)S(1)}, bf16[3,3,128,128]{3,2,1,0:T(8,128)(2,1)}, u32[]{:S(2)}) copy-start(bf16[3,3,128,128]{3,2,1,0:T(8,128)(2,1)} %param.8) | copy-start | bytes 884740
  83.9 25.5 %all-to-all-start.2 = ((bf16[128,24,128]{2,1,0:T(8,128)(2,1)}), bf16[128,24,128]{2,1,0:T(8,128)(2,1)S(1)}, u32[]{:S(2)}, u32[]{:S(2)}) async-start(bf16[128,24,128]{2,1,0:T(8,128)(2,1)} %broadcast_in_dim.10), calls=%async_computation.2 | async-start | bytes 1572864 | tf_op jit(solution)/shard_map/all_to_all | solution.py:364

commit v2 on v1

v2 whole, which is shorter than its diff:
```python
import jax
import jax.numpy as jnp
from jax import lax
from jax.experimental import pallas as pl
from jax.experimental.pallas import tpu as pltpu
from jax.sharding import PartitionSpec as P

POOL = 8
AXES = ("lat", "lon")
ROWS, COLS, DEPTH = 16, 48, 128
WIDE = 512
STRIDE = 64
EXT = 21 * STRIDE
RIM = 19 * STRIDE
OWN = ROWS * STRIDE
CROW, CCOL = ROWS // POOL, COLS // POOL
NLAT, NLON = 8, 16
COUNT = NLAT * NLON
GROW, GCOL = NLAT * CROW, NLON * CCOL
CELLS = GROW * GCOL
PACK = 2 * CROW * CCOL
WIN = 16
F32 = jnp.float32
BF16 = jnp.bfloat16


def mm(left, right, contract=((1,), (0,))):
    return lax.dot_general(left, right, (contract, ((), ())), preferred_element_type=F32)


def side_by_side(flat):
    wide = flat.astype(F32)
    low = pltpu.roll(wide, 1, 0).astype(BF16)
    high = pltpu.roll(wide, flat.shape[0] - 1, 0).astype(BF16)
    return jnp.concatenate([low, flat.astype(BF16), high], axis=1)


def split_two(value):
    high = value.astype(BF16)
    return high, (value - high.astype(F32)).astype(BF16)


def rim_position(shape, dim):
    spot = lax.broadcasted_iota(jnp.int32, shape, dim)
    slot = spot & (STRIDE - 1)
    line = spot >> 6
    left = slot == STRIDE - 1
    row = jnp.where(left, line - 1, line - 2)
    col = jnp.where(left, -1, slot)
    return row, col


def row_live(row, lat):
    return jnp.logical_and(
        jnp.logical_or(row >= 0, lat > 0), jnp.logical_or(row < ROWS, lat < NLAT - 1)
    )


def mirrored(kernel, tap):
    base = 3 * (2 - tap)
    return jnp.concatenate([kernel[base + 2], kernel[base + 1], kernel[base]], axis=1)


def first_kernel(
    pos, got_inner, got_outer, strip, fine, grad, w_enc_far, w_dec_far,
    pack_out, hid_out, slope_out, dm_out, field_out,
    pack, field, grad_field, fine_cat, grad_cat, hid_here, slope_here, dm_here, w_enc, w_dec, sems,
):
    lat = pos[0]
    even = lat % 2 == 0
    fetches = [
        pltpu.make_async_copy(a, b, sems.at[5 + k])
        for k, (a, b) in enumerate(
            (
                (fine, field.at[3:19, 0:COLS, :]),
                (grad, grad_field.at[3:19, 0:COLS, :]),
                (w_enc_far, w_enc),
                (w_dec_far, w_dec),
            )
        )
    ]
    for fetch in fetches:
        fetch.start()
    sources = (field, hid_here, slope_here, dm_here, pack)
    targets = (field_out, hid_out, slope_out, dm_out, pack_out)
    copies = [
        pltpu.make_async_copy(a, b, sems.at[k]) for k, (a, b) in enumerate(zip(sources, targets))
    ]
    for part, (space, cat) in enumerate(((field, fine_cat), (grad_field, grad_cat))):
        lanes = slice(part * DEPTH, (part + 1) * DEPTH)
        space[0:1, 0:COLS, :] = jnp.zeros((1, COLS, DEPTH), BF16)
        inner = got_inner[2 * part : 2 * part + 2]
        outer = got_outer[2 * part : 2 * part + 2]
        space[1:3, 0:COLS, :] = jnp.where(even, outer, inner)
        space[19:21, 0:COLS, :] = jnp.where(even, inner, outer)
        space[:, COLS:STRIDE, :] = strip[:, :, lanes]
        fetches[part].wait()
        if part == 0:
            copies[0].start()
        cat[...] = side_by_side(space[...].reshape(EXT, DEPTH))
    act = jnp.zeros((RIM, DEPTH), F32)
    fetches[2].wait()
    for tap in range(3):
        act = act + mm(fine_cat[tap * STRIDE : tap * STRIDE + RIM, :], w_enc[tap])
    row, _ = rim_position((RIM, 1), 0)
    live = row_live(row, lat)
    sig = jax.nn.sigmoid(act)
    hid = jnp.where(live, act * sig, 0.0).astype(BF16)
    hid_here[...] = hid
    copies[1].start()
    slope_here[...] = jnp.where(live, sig * (1.0 + act * (1.0 - sig)), 0.0)
    copies[2].start()
    dm = jnp.zeros((RIM, DEPTH), F32)
    fetches[3].wait()
    for tap in range(3):
        dm = dm + mm(
            grad_cat[tap * STRIDE : tap * STRIDE + RIM, :], mirrored(w_dec, tap), ((1,), (1,))
        )
    dm_here[...] = dm
    copies[3].start()
    half = PACK // 2
    prow, pcol = rim_position((PACK, RIM), 1)
    which = lax.broadcasted_iota(jnp.int32, (PACK, RIM), 0)
    inside = (prow >= 0) & (prow < ROWS) & (pcol >= 0) & (pcol < COLS)
    cell = jnp.where(inside, (prow >> 3) * CCOL + (pcol >> 3), -1)
    take_hid = (cell == which).astype(F32).astype(BF16)
    take_dm = (inside & (cell + half == which)).astype(F32).astype(BF16)
    dm_high, dm_low = split_two(dm)
    packed = mm(take_hid, hid) * (1.0 / (POOL * POOL)) + (mm(take_dm, dm_high) + mm(take_dm, dm_low))
    packed = packed.astype(BF16)
    for peer in range(COUNT):
        pack[peer] = packed
    copies[4].start()
    for copy in copies:
        copy.wait()


def weight_kernel(w_down, w_bot, out):
    out[0] = mm(w_down[...], w_bot[0]).astype(BF16)


def third(value):
    return (value * 43) >> 8


def source_of(row, col, shift):
    inside = (row >= 0) & (row < GROW)
    col = jnp.where(col < 0, col + GCOL, col)
    col = jnp.where(col >= GCOL, col - GCOL, col)
    group = third(col)
    device = (row >> 1) * NLON + group
    return jnp.where(inside, device * PACK + shift + (row & 1) * CCOL + (col - group * CCOL), -1)


def second_kernel(
    pos, every, w_up, w_eff_far, hid_far, slope_far, dm_far, field_far, grad_far,
    parts_out, merged_out, dact_out,
    parts, w_eff, hid, slope, dm, field, own_grad, fine_cat, merged_cat, merged_here, dact_here, sems,
):
    lat, lon = pos[0], pos[1]
    fetches = [
        pltpu.make_async_copy(a, b, sems.at[k])
        for k, (a, b) in enumerate(
            (
                (w_eff_far, w_eff),
                (field_far, field),
                (hid_far, hid),
                (dm_far, dm),
                (slope_far, slope),
                (grad_far, own_grad.at[:, 0:COLS, :]),
            )
        )
    ]
    stores = [
        pltpu.make_async_copy(merged_here, merged_out, sems.at[6]),
        pltpu.make_async_copy(dact_here, dact_out, sems.at[7]),
        pltpu.make_async_copy(parts.at[0:1152, :], parts_out.at[0:1152, :], sems.at[8]),
        pltpu.make_async_copy(parts.at[1152:, :], parts_out.at[1152:, :], sems.at[9]),
    ]
    for fetch in fetches:
        fetch.start()
    own_grad[:, COLS:, :] = jnp.zeros((ROWS, STRIDE - COLS, DEPTH), BF16)
    spot = lax.broadcasted_iota(jnp.int32, (8 * WIN, 1), 0)
    line, slot = spot >> 4, spot & (WIN - 1)
    src = source_of(CROW * lat + line - 3, CCOL * lon + slot - 3, 0)
    src = jnp.where(slot < CCOL + 6, src, -1)
    spot = lax.broadcasted_iota(jnp.int32, (6 * WIN, 1), 0)
    line, slot = spot >> 4, spot & (WIN - 1)
    dsrc = source_of(CROW * lat + line - 2, CCOL * lon + slot - 2, CROW * CCOL)
    dsrc = jnp.where(slot < CCOL + 4, dsrc, -1)
    reach = 5 * NLON * PACK
    begin = jnp.clip(lat - 2, 0, NLAT - 5) * (NLON * PACK)
    near = every[pl.ds(pl.multiple_of(begin, NLON * PACK), reach), :]
    spots = lax.broadcasted_iota(jnp.int32, (8 * WIN, reach), 1) + begin
    pooled = mm((spots == src).astype(F32).astype(BF16), near)
    spots = lax.broadcasted_iota(jnp.int32, (6 * WIN, reach), 1) + begin
    dlift = mm((spots == dsrc).astype(F32).astype(BF16), near).astype(BF16)
    shifted = [pooled.astype(BF16)] + [
        pltpu.roll(pooled, 8 * WIN - step, 0).astype(BF16) for step in (1, 2)
    ]
    pooled_cat = jnp.concatenate(shifted, axis=1)
    zpre = jnp.zeros((6 * WIN, WIDE), F32)
    fetches[0].wait()
    for tap in range(3):
        zpre = zpre + mm(
            pooled_cat[tap * WIN : tap * WIN + 6 * WIN], w_eff[tap * 384 : tap * 384 + 384, :]
        )
    sig = jax.nn.sigmoid(zpre)
    zact = (zpre * sig).astype(BF16)
    dz = mm(dlift, w_up[...], ((1,), (1,))) * (sig * (1.0 + zpre * (1.0 - sig)))
    dz = dz.astype(BF16)
    lifted = mm(zact, w_up[...])
    taps = mm(dz, w_eff[...], ((1,), (1,)))
    dpool = jnp.zeros((6 * WIN, DEPTH), F32)
    for tap_a in range(3):
        for tap_b in range(3):
            spot = ((2 - tap_a) * 3 + (2 - tap_b)) * DEPTH
            turn = ((1 - tap_a) * WIN + (1 - tap_b)) % (6 * WIN)
            part = taps[:, spot : spot + DEPTH]
            dpool = dpool + (part if turn == 0 else pltpu.roll(part, turn, 0))
    dpool = dpool * (1.0 / (POOL * POOL))
    lift_high, lift_low = split_two(lifted)
    pool_high, pool_low = split_two(dpool)
    tail = jnp.zeros((2 * WIN, 2 * DEPTH), BF16)
    table = jnp.concatenate(
        [
            jnp.concatenate([lift_high, pool_high], axis=1),
            tail,
            jnp.concatenate([lift_low, pool_low], axis=1),
            tail,
        ],
        axis=0,
    )
    row, col = rim_position((RIM, 1), 0)
    home = (((row + POOL) >> 3) + 1) * WIN + ((col + POOL) >> 3) + 1
    home = jnp.where(col <= COLS, home, -1)
    cells = lax.broadcasted_iota(jnp.int32, (RIM, 256), 1) & 127
    spread = mm((cells == home).astype(F32).astype(BF16), table)
    live = row_live(row, lat)
    for fetch in fetches[1:]:
        fetch.wait()
    merged = jnp.where(live, hid[...].astype(F32) + spread[:, :DEPTH], 0.0)
    dact = (dm[...] + spread[:, DEPTH:]) * slope[...]
    merged_here[...] = merged.astype(BF16)
    stores[0].start()
    dact_here[...] = dact.astype(BF16)
    stores[1].start()
    merged_cat[...] = side_by_side(merged.astype(BF16))
    fine_cat[...] = side_by_side(field[...].reshape(EXT, DEPTH))
    slot = lax.broadcasted_iota(jnp.int32, (OWN, 1), 0) & (STRIDE - 1)
    center = dact_here[2 * STRIDE : 2 * STRIDE + OWN, :]
    own_dact = jnp.where(slot < COLS, center, jnp.zeros_like(center))
    center_grad = own_grad[...].reshape(OWN, DEPTH)
    for tap in range(3):
        start = (tap + 1) * STRIDE
        parts[tap * 384 : tap * 384 + 384, :] = mm(
            merged_cat[start : start + OWN, :], center_grad, ((0,), (0,))
        ).astype(BF16)
    stores[2].start()
    for tap in range(3):
        start = (tap + 2) * STRIDE
        parts[1152 + tap * 384 : 1152 + tap * 384 + 384, :] = mm(
            fine_cat[start : start + OWN, :], own_dact, ((0,), (0,))
        ).astype(BF16)
    stores[3].start()
    for store in stores:
        store.wait()


def third_kernel(merged, dact, w_dec, w_enc, block_out, field_grad, merged_cat, dact_cat):
    merged_cat[...] = side_by_side(merged[...])
    dact_cat[...] = side_by_side(dact[...])
    out = jnp.zeros((OWN, DEPTH), F32)
    back = jnp.zeros((OWN, DEPTH), F32)
    for tap in range(3):
        start = (tap + 1) * STRIDE
        out = out + mm(merged_cat[start : start + OWN, :], w_dec[tap])
        back = back + mm(dact_cat[start : start + OWN, :], mirrored(w_enc, tap), ((1,), (1,)))
    block_out[...] = out.astype(BF16).reshape(ROWS, STRIDE, DEPTH)[:, :COLS, :]
    field_grad[...] = back.astype(BF16).reshape(ROWS, STRIDE, DEPTH)[:, :COLS, :]


def coarse_kernel(every, w_eff, w_up, table, g_up, pooled_cat, dlift, zact, dz):
    line = 2 * GCOL
    block = NLON * PACK
    spot = lax.broadcasted_iota(jnp.int32, (4 * line, 1), 0)
    kind = (spot >= line).astype(jnp.int32) + (spot >= 2 * line).astype(jnp.int32)
    kind = kind + (spot >= 3 * line).astype(jnp.int32)
    within = spot - kind * line
    row = (within >= GCOL).astype(jnp.int32)
    col = within - row * GCOL
    col = jnp.where(kind < 3, col + kind - 1, col)
    shift = jnp.where(kind < 3, 0, CROW * CCOL)
    src = source_of(row, col, shift)
    spots = lax.broadcasted_iota(jnp.int32, (4 * line, block), 1)
    order = (spots == src).astype(F32).astype(BF16)
    edge = jnp.zeros((GCOL, 3 * DEPTH), BF16)
    pooled_cat[0:GCOL, :] = edge
    pooled_cat[(GROW + 1) * GCOL :, :] = edge
    for pair in range(NLAT // 2):
        both = jnp.concatenate(
            [every[(2 * pair + k) * block : (2 * pair + k + 1) * block, :] for k in (0, 1)],
            axis=1,
        )
        moved = mm(order, both).astype(BF16)
        for k in (0, 1):
            lat = 2 * pair + k
            lanes = slice(k * DEPTH, (k + 1) * DEPTH)
            at = GCOL + lat * line
            for b in range(3):
                pooled_cat[at : at + line, b * DEPTH : (b + 1) * DEPTH] = moved[
                    b * line : (b + 1) * line, lanes
                ]
            dlift[lat * line : (lat + 1) * line, :] = moved[3 * line :, lanes]
    for part in range(NLAT):
        base = part * line
        zpre = jnp.zeros((line, WIDE), F32)
        for tap in range(3):
            at = base + tap * GCOL
            zpre = zpre + mm(pooled_cat[at : at + line, :], w_eff[tap * 384 : tap * 384 + 384, :])
        sig = jax.nn.sigmoid(zpre)
        zact[base : base + line, :] = (zpre * sig).astype(BF16)
        up = mm(dlift[base : base + line, :], w_up[...], ((1,), (1,)))
        dz[base : base + line, :] = (up * (sig * (1.0 + zpre * (1.0 - sig)))).astype(BF16)
    g_up[...] = mm(zact[...], dlift[...], ((0,), (0,)))
    for tap in range(3):
        at = tap * GCOL
        corr = mm(pooled_cat[at : at + CELLS, :], dz[...], ((0,), (0,)))
        high, low = split_two(corr)
        for b in range(3):
            lanes = slice(b * DEPTH, (b + 1) * DEPTH)
            table[tap * 3 + b, 0:DEPTH, :] = high[lanes]
            table[tap * 3 + b, DEPTH:, :] = low[lanes]


def remainder(value):
    return value - 18 * ((value * 3641) >> 16)


def fold_kernel(spread, out):
    full = COUNT * 18
    slot = remainder(lax.broadcasted_iota(jnp.int32, (32, full), 1))
    pick = slot == lax.broadcasted_iota(jnp.int32, (32, full), 0)
    total = mm(pick.astype(F32).astype(BF16), spread[...]).astype(BF16)
    slot = remainder(lax.broadcasted_iota(jnp.int32, (full, 1), 0))
    copy = lax.broadcasted_iota(jnp.int32, (full, 32), 1) == slot
    out[...] = mm(copy.astype(F32).astype(BF16), total).astype(BF16)


def finish_kernel(whole, g_dec, g_enc):
    g_dec[...] = whole[:1152].astype(F32)
    g_enc[...] = whole[1152:].astype(F32)


def tail_kernel(table, w_down, w_bot, g_bot, g_down):
    step = pl.program_id(0)

    @pl.when(step == 0)
    def _():
        g_down[...] = jnp.zeros((DEPTH, WIDE), F32)

    pair = table[0]
    twice = jnp.concatenate([w_down[...], w_down[...]], axis=0)
    g_bot[0] = mm(twice, pair, ((0,), (0,)))
    back = mm(pair, w_bot[0], ((1,), (1,)))
    g_down[...] += back[:DEPTH] + back[DEPTH:]


def vmem():
    return pl.BlockSpec(memory_space=pltpu.VMEM)


def far():
    return pl.BlockSpec(memory_space=pltpu.HBM)


def smem():
    return pl.BlockSpec(memory_space=pltpu.SMEM)


def shape(dims, kind):
    return jax.ShapeDtypeStruct(dims, kind)


def held(value):
    return pltpu.with_memory_space_constraint(value, pltpu.HBM)


def grant(mib):
    return pltpu.CompilerParams(vmem_limit_bytes=mib * 1024 * 1024)


def body(fine, w_enc, w_down, w_bot, w_up, w_dec, grad):
    pos = jnp.stack([lax.axis_index("lat"), lax.axis_index("lon")]).astype(jnp.int32)
    inner = [(i, i ^ 1) for i in range(NLAT)]
    outer = [(i, ((i + 1) ^ 1) - 1) for i in range(1, NLAT - 1)]
    even = lax.axis_index("lat") % 2 == 0
    right = [(i, (i + 1) % NLON) for i in range(NLON)]
    left = [(t, s) for s, t in right]
    under = jnp.concatenate([fine[-2:], grad[-2:]], axis=0)
    over = jnp.concatenate([fine[:2], grad[:2]], axis=0)
    got_inner = lax.ppermute(jnp.where(even, under, over), "lat", inner)
    got_outer = lax.ppermute(jnp.where(even, over, under), "lat", outer)
    top = jnp.where(even, got_outer, got_inner)
    bot = jnp.where(even, got_inner, got_outer)

    def edge(cols):
        return jnp.concatenate(
            [
                jnp.concatenate([top[at : at + 2, cols], tile[:, cols], bot[at : at + 2, cols]], axis=0)
                for at, tile in ((0, fine), (2, grad))
            ],
            axis=2,
        )

    first = edge(slice(0, 2))
    last = edge(slice(COLS - 2, COLS))
    high = lax.ppermute(first, "lon", left)
    low = lax.ppermute(last, "lon", right)
    strip = jnp.concatenate(
        [
            jnp.pad(high, ((1, 0), (0, 0), (0, 0))),
            jnp.zeros((21, 12, 2 * DEPTH), BF16),
            jnp.pad(low, ((0, 1), (0, 0), (0, 0))),
        ],
        axis=1,
    )
    w_eff = pl.pallas_call(
        weight_kernel,
        grid=(9,),
        in_specs=[
            pl.BlockSpec((DEPTH, WIDE), lambda i: (0, 0)),
            pl.BlockSpec((1, WIDE, WIDE), lambda i: (i, 0, 0)),
        ],
        out_specs=pl.BlockSpec((1, DEPTH, WIDE), lambda i: (i, 0, 0)),
        out_shape=shape((9, DEPTH, WIDE), BF16),
        name="weights",
        compiler_params=grant(56),
    )(w_down, w_bot.reshape(9, WIDE, WIDE)).reshape(9 * DEPTH, WIDE)
    w_enc_f = w_enc.reshape(3, 3 * DEPTH, DEPTH)
    w_dec_f = w_dec.reshape(3, 3 * DEPTH, DEPTH)
    pack, hid, slope, dm, field = pl.pallas_call(
        first_kernel,
        in_specs=[smem()] + [vmem()] * 3 + [far()] * 4,
        out_specs=[far()] * 5,
        out_shape=[
            pltpu.HBM((COUNT, PACK, DEPTH), BF16),
            pltpu.HBM((RIM, DEPTH), BF16),
            pltpu.HBM((RIM, DEPTH), F32),
            pltpu.HBM((RIM, DEPTH), F32),
            pltpu.HBM((21, STRIDE, DEPTH), BF16),
        ],
        scratch_shapes=[
            pltpu.VMEM((COUNT, PACK, DEPTH), BF16),
            pltpu.VMEM((21, STRIDE, DEPTH), BF16),
            pltpu.VMEM((21, STRIDE, DEPTH), BF16),
            pltpu.VMEM((EXT, 3 * DEPTH), BF16),
            pltpu.VMEM((EXT, 3 * DEPTH), BF16),
            pltpu.VMEM((RIM, DEPTH), BF16),
            pltpu.VMEM((RIM, DEPTH), F32),
            pltpu.VMEM((RIM, DEPTH), F32),
            pltpu.VMEM((3, 3 * DEPTH, DEPTH), BF16),
            pltpu.VMEM((9, DEPTH, DEPTH), BF16),
            pltpu.SemaphoreType.DMA((9,)),
        ],
        name="first",
        compiler_params=grant(30),
    )(
        pos, got_inner, got_outer, strip,
        *(held(x) for x in (fine, grad, w_enc_f, w_dec.reshape(9, DEPTH, DEPTH))),
    )
    every = lax.all_to_all(pack, AXES, 0, 0).reshape(COUNT * PACK, DEPTH)
    parts, merged, dact = pl.pallas_call(
        second_kernel,
        in_specs=[smem(), vmem(), vmem()] + [far()] * 6,
        out_specs=[far()] * 3,
        out_shape=[
            pltpu.HBM((2304, DEPTH), BF16),
            pltpu.HBM((RIM, DEPTH), BF16),
            pltpu.HBM((RIM, DEPTH), BF16),
        ],
        scratch_shapes=[
            pltpu.VMEM((2304, DEPTH), BF16),
            pltpu.VMEM((9 * DEPTH, WIDE), BF16),
            pltpu.VMEM((RIM, DEPTH), BF16),
            pltpu.VMEM((RIM, DEPTH), F32),
            pltpu.VMEM((RIM, DEPTH), F32),
            pltpu.VMEM((21, STRIDE, DEPTH), BF16),
            pltpu.VMEM((ROWS, STRIDE, DEPTH), BF16),
            pltpu.VMEM((EXT, 3 * DEPTH), BF16),
            pltpu.VMEM((RIM, 3 * DEPTH), BF16),
            pltpu.VMEM((RIM, DEPTH), BF16),
            pltpu.VMEM((RIM, DEPTH), BF16),
            pltpu.SemaphoreType.DMA((10,)),
        ],
        name="second",
        compiler_params=grant(30),
    )(pos, every, w_up, *(held(x) for x in (w_eff, hid, slope, dm, field, grad)))
    parts, later, merged, dact = lax.optimization_barrier(
        (parts, every, merged, dact)
    )
    spread = lax.all_to_all(parts.reshape(COUNT, 9, 2, DEPTH), AXES, 0, 0)
    table, g_up = pl.pallas_call(
        coarse_kernel,
        in_specs=[vmem()] * 3,
        out_specs=[vmem()] * 2,
        out_shape=[
            shape((9, 2 * DEPTH, WIDE), BF16),
            shape((WIDE, DEPTH), F32),
        ],
        scratch_shapes=[
            pltpu.VMEM(((GROW + 2) * GCOL, 3 * DEPTH), BF16),
            pltpu.VMEM((CELLS, DEPTH), BF16),
            pltpu.VMEM((CELLS, WIDE), BF16),
            pltpu.VMEM((CELLS, WIDE), BF16),
        ],
        name="coarse",
        compiler_params=grant(56),
    )(later, w_eff, w_up)
    block_out, field_grad = pl.pallas_call(
        third_kernel,
        in_specs=[vmem()] * 4,
        out_specs=[vmem()] * 2,
        out_shape=[shape((ROWS, COLS, DEPTH), BF16)] * 2,
        scratch_shapes=[pltpu.VMEM((RIM, 3 * DEPTH), BF16)] * 2,
        name="third",
        compiler_params=grant(56),
    )(merged, dact, w_dec_f, w_enc.reshape(9, DEPTH, DEPTH))
    spread, table, block_out = lax.optimization_barrier((spread, table, block_out))
    total = pl.pallas_call(
        fold_kernel,
        in_specs=[vmem()],
        out_specs=vmem(),
        out_shape=pltpu.VMEM((2304, DEPTH), BF16),
        name="fold",
        compiler_params=grant(8),
    )(spread.reshape(2304, DEPTH))
    total, table = lax.optimization_barrier((total, table))
    whole = lax.all_to_all(total.reshape(COUNT, 9, 2, DEPTH), AXES, 0, 0)
    g_bot, g_down = pl.pallas_call(
        tail_kernel,
        grid=(9,),
        in_specs=[
            pl.BlockSpec((1, 2 * DEPTH, WIDE), lambda i: (i, 0, 0)),
            pl.BlockSpec((DEPTH, WIDE), lambda i: (0, 0)),
            pl.BlockSpec((1, WIDE, WIDE), lambda i: (i, 0, 0)),
        ],
        out_specs=[
            pl.BlockSpec((1, WIDE, WIDE), lambda i: (i, 0, 0)),
            pl.BlockSpec((DEPTH, WIDE), lambda i: (0, 0)),
        ],
        out_shape=[shape((9, WIDE, WIDE), F32), shape((DEPTH, WIDE), F32)],
        name="tail",
        compiler_params=grant(56),
    )(table, w_down, w_bot.reshape(9, WIDE, WIDE))
    whole, g_bot = lax.optimization_barrier((whole, g_bot))
    g_dec, g_enc = pl.pallas_call(
        finish_kernel,
        in_specs=[vmem()],
        out_specs=[vmem()] * 2,
        out_shape=[shape((1152, DEPTH), F32)] * 2,
        name="finish",
        compiler_params=grant(6),
    )(whole.reshape(2304, DEPTH))
    g_dec = g_dec.reshape(3, 3, DEPTH, DEPTH)
    g_enc = g_enc.reshape(3, 3, DEPTH, DEPTH)
    return (block_out, field_grad, g_enc, g_down, g_bot.reshape(3, 3, WIDE, WIDE), g_up, g_dec)


def solution(mesh):
    return jax.shard_map(
        body,
        mesh=mesh,
        in_specs=(P("lat", "lon", None), P(), P(), P(), P(), P(), P("lat", "lon", None)),
        out_specs=(P("lat", "lon", None), P("lat", "lon", None), P(), P(), P(), P(), P()),
        check_vma=False,
    )
```

time: 112 us -> 99.4 us (0.89)
  blocking collectives: 21.2 us -> 0 us
  starting transfers between devices: 23.9 us -> 32.3 us
  local copies, waits for them, and re-layouts: 6.83 us -> 1.75 us
  Pallas kernels: 39.9 us -> 44.1 us
  waiting for transfers between devices: 15.3 us -> 19.4 us
  other arithmetic: 3.31 us -> 0.24 us
    all_to_all x1 -> x0, blocking collectives: 21.2 us -> none  [body(): spread = lax.all_to_all(parts.reshape(COUNT, PACK, DEPTH), AXES, 0, 0)]
    all_to_all x1 -> x2, starting transfers between devices: 4.19 us -> 11.9 us  [the longest x1 7.72 us: body(): whole = lax.all_to_all(total.reshape(COUNT, 9, 2, DEPTH), AXES, 0, 0)]
    all_to_all x1 -> x2, waiting for transfers between devices: 0.01 us -> 5.84 us  [the longest x1 3.66 us: body(): whole = lax.all_to_all(total.reshape(COUNT, 9, 2, DEPTH), AXES, 0, 0)]
    pallas_call x3 -> x6, Pallas kernels: 28.8 us -> 33.4 us  [the longest x1 11 us: body(): pl.pallas_call(tail_kernel, grid=(9,), in_specs=[pl.BlockSpec((1, 2 * DEP...]
    ppermute x2, waiting for transfers between devices: 4.01 us -> 1.04 us  [the longest x1 1.04 us: body(): got_inner = lax.ppermute(jnp.where(even, under, over), 'lat', inner)]
    transpose x4 -> x0, local copies, waits for them, and re-layouts: 2.79 us -> none  [turned(): flipped = jnp.flip(kernel, (0, 1)).swapaxes(2, 3)]
    unnamed x9 -> x4, local copies, waits for them, and re-layouts: 1.88 us -> 0.01 us
    convert_element_type x2 -> x0, other arithmetic: 1.72 us -> none  [the longest x1 0.86 us: body(): g_enc = whole[1152:2304].astype(F32).reshape(3, 3, DEPTH, DEPTH)]
  transfers between devices with their start and end apart: 6 -> 7, of which waited for: 3 -> 6; matrix products, arithmetic and copies ran while one was open for 3% -> 1% of each run, Pallas kernels for 25% -> 31%
where the time goes in v2:
time: 99.4 us; the launch traced here: 98.6 us
  Pallas kernels  44.1 us (44%)
  starting transfers between devices  32.3 us (32%)
  waiting for transfers between devices  19.4 us (20%)
  local copies, waits for them, and re-layouts  1.75 us (2%)
    pallas_call x1, Pallas kernels, body(): pl.pallas_call(tail_kernel, grid=(9,), in_specs=[pl.BlockSpec((1, 2 * DEP...  11 us
    all_to_all x1, starting transfers between devices, body(): every = lax.all_to_all(pack, AXES, 0, 0).reshape(COUNT * PACK, DEPTH)  10.1 us
    pallas_call x1, Pallas kernels, body(): pl.pallas_call(coarse_kernel, in_specs=[vmem()] * 3, out_specs=[vmem()] *...  9.26 us
    all_to_all x1, waiting for transfers between devices, body(): every = lax.all_to_all(pack, AXES, 0, 0).reshape(COUNT * PACK, DEPTH)  9.21 us
    all_to_all x1, starting transfers between devices, body(): whole = lax.all_to_all(total.reshape(COUNT, 9, 2, DEPTH), AXES, 0, 0)  7.72 us
    pallas_call x1, Pallas kernels, body(): pl.pallas_call(weight_kernel, grid=(9,), in_specs=[pl.BlockSpec((DEPTH, W...  7.41 us
    ppermute x1, starting transfers between devices, body(): got_inner = lax.ppermute(jnp.where(even, under, over), 'lat', inner)  6.47 us
    pallas_call x1, Pallas kernels, body(): pl.pallas_call(second_kernel, in_specs=[smem(), vmem(), vmem()] + [far()]...  5.64 us
  transfers between devices with their start and end apart: 7, of which 6 were waited for; matrix products, arithmetic and copies ran while one was open for 1% of the time, Pallas kernels for 31%

profile of v2, /device:TPU:1, one launch (start us, length us, event | category | flops | bytes accessed | tf_op | source)
XLA Modules:
  0.0 98.6 jit_solution(7083676400476828522)
XLA Ops:
  0.6 0.8 fusion.6
  1.5 0.7 collective-permute-start.1
  2.1 6.5 %collective-permute-start = (bf16[4,48,128]{2,1,0:T(8,128)(2,1)S(1)}, bf16[4,48,128]{2,1,0:T(8,128)(2,1)S(1)}, u32[]{:S(2)}, u32[]{:S(2)}) collective-permute-start(bf16[4,48,128]{2,1,0:T(8,128)(2,1)S(1)} %get-tuple-element.72), channel_id=1, source_target_pairs={{0,16},{16,0},{32,48},{48,32},{64,80},{80,64},{96,112},{112,96},{1... | collective-permute-start | bytes 147464 | tf_op jit(solution)/shard_map/ppermute | solution.py:402
  8.6 0.8 fusion.4
  9.5 1.0 %collective-permute-done.got_inner = bf16[4,48,128]{2,1,0:T(8,128)(2,1)S(1)} collective-permute-done((bf16[4,48,128]{2,1,0:T(8,128)(2,1)S(1)}, bf16[4,48,128]{2,1,0:T(8,128)(2,1)S(1)}, u32[]{:S(2)}, u32[]{:S(2)}) %collective-permute-start) | collective-permute-done | bytes 49184 | tf_op jit(solution)/shard_map/ppermute | solution.py:402
  10.6 3.0 %collective-permute-start.3 = (bf16[20,2,256]{2,1,0:T(2,128)(2,1)S(1)}, bf16[20,2,256]{2,1,0:T(2,128)(2,1)S(1)}, u32[]{:S(2)}, u32[]{:S(2)}) collective-permute-start(bf16[20,2,256]{2,1,0:T(2,128)(2,1)S(1)} %maximum_maximum_fusion.1), channel_id=1, source_target_pairs={{0,1},{1,2},{2,3},{3,4},{4,5},{5,6},{6,7},{7,8},{8,9},{9,10},{10,1... | collective-permute-start | bytes 61448 | tf_op jit(solution)/shard_map/ppermute | solution.py:419
  13.7 0.1 pad_add_fusion.pos
  13.8 0.6 collective-permute-done.3
  14.5 2.7 %collective-permute-done.2 = bf16[20,2,256]{2,1,0:T(2,128)(2,1)S(1)} collective-permute-done((bf16[20,2,256]{2,1,0:T(2,128)(2,1)S(1)}, bf16[20,2,256]{2,1,0:T(2,128)(2,1)S(1)}, u32[]{:S(2)}, u32[]{:S(2)}) %collective-permute-start.2) | collective-permute-done | bytes 20512 | tf_op jit(solution)/shard_map/ppermute | solution.py:418
  17.2 0.1 fusion.2.strip
  17.3 5.1 %first.1 = (bf16[128,24,128]{2,1,0:T(8,128)(2,1)}, bf16[1216,128]{1,0:T(8,128)(2,1)}, f32[1216,128]{1,0:T(8,128)}, f32[1216,128]{1,0:T(8,128)}, bf16[21,64,128]{2,1,0:T(8,128)(2,1)}) custom-call(s32[2]{0:T(128)S(1)} %pad_add_fusion.pos, bf16[4,48,128]{2,1,0:T(8,128)(2,1)S(1)} %collective-permute-done.got_inner, ...), custom_call_target="tpu_custom_call" | custom-call | tf_op jit(solution)/shard_map/first/pallas_call | solution.py:442
  22.3 10.1 %all-to-all-start = ((bf16[128,24,128]{2,1,0:T(8,128)(2,1)}), bf16[128,24,128]{2,1,0:T(8,128)(2,1)S(1)}, u32[]{:S(2)}, u32[]{:S(2)}) async-start(bf16[128,24,128]{2,1,0:T(8,128)(2,1)} %get-tuple-element.34), calls=%async_computation | async-start | bytes 1572864 | tf_op jit(solution)/shard_map/all_to_all | solution.py:472
  32.5 7.4 %weights.1 = bf16[9,128,512]{2,1,0:T(8,128)(2,1)} custom-call(bf16[128,512]{1,0:T(8,128)(2,1)} %w_down.3, bf16[9,512,512]{2,1,0:T(8,128)(2,1)} %bitcast.20), custom_call_target="tpu_custom_call" | custom-call | tf_op jit(solution)/shard_map/weights/pallas_call | solution.py:428
  39.9 9.2 %all-to-all-done = bf16[128,24,128]{2,1,0:T(8,128)(2,1)S(1)} async-done(((bf16[128,24,128]{2,1,0:T(8,128)(2,1)}), bf16[128,24,128]{2,1,0:T(8,128)(2,1)S(1)}, u32[]{:S(2)}, u32[]{:S(2)}) %all-to-all-start) | async-done | bytes 786464 | tf_op jit(solution)/shard_map/all_to_all | solution.py:472
  49.1 5.6 %second.1 = (bf16[2304,128]{1,0:T(8,128)(2,1)}, bf16[1216,128]{1,0:T(8,128)(2,1)}, bf16[1216,128]{1,0:T(8,128)(2,1)}) custom-call(s32[2]{0:T(128)S(1)} %pad_add_fusion.pos, bf16[3072,128]{1,0:T(8,128)(2,1)S(1)} %bitcast.16, bf16[512,128]{1,0:T(8,128)(2,1)S(1)} %copy-done.1, bf16[1152,512]{1,0:T(8,128)(2,1)} %bitcast.22, ...), custom_call_target="tpu_custom_call" | custom-call | tf_op jit(solution)/shard_map/second/pallas_call | solution.py:473
  54.7 4.2 %all-to-all-start.1 = ((bf16[128,9,2,128]{3,2,1,0:T(2,128)(2,1)}), bf16[128,9,2,128]{3,2,1,0:T(2,128)(2,1)S(1)}, u32[]{:S(2)}, u32[]{:S(2)}) async-start(bf16[128,9,2,128]{3,2,1,0:T(2,128)(2,1)} %bitcast.28), calls=%async_computation.1 | async-start | bytes 1179648 | tf_op jit(solution)/shard_map/all_to_all | solution.py:502
  59.0 9.3 %coarse.1 = (bf16[9,256,512]{2,1,0:T(8,128)(2,1)}, f32[512,128]{1,0:T(8,128)}) custom-call(bf16[3072,128]{1,0:T(8,128)(2,1)} %bitcast.17, bf16[1152,512]{1,0:T(8,128)(2,1)} %bitcast.23, bf16[512,128]{1,0:T(8,128)(2,1)} %w_up.3), custom_call_target="tpu_custom_call" | custom-call | tf_op jit(solution)/shard_map/coarse/pallas_call | solution.py:503
  68.2 3.3 %third.1 = (bf16[16,48,128]{2,1,0:T(8,128)(2,1)}, bf16[16,48,128]{2,1,0:T(8,128)(2,1)}) custom-call(bf16[1216,128]{1,0:T(8,128)(2,1)} %get-tuple-element.45.merged, bf16[1216,128]{1,0:T(8,128)(2,1)} %get-tuple-element.46.dact, bf16[3,384,128]{2,1,0:T(8,128)(2,1)} %bitcast.27, bf16[9,128,128]{2,1,0:T(8,128)(2,1)} %bitcast.25), custom_call_target="tpu_custom_call" | custom-call | tf_op jit(solution)/shard_map/third/pallas_call | solution.py:520
  71.6 2.2 %all-to-all-done.1 = bf16[128,9,2,128]{3,2,1,0:T(2,128)(2,1)S(1)} async-done(((bf16[128,9,2,128]{3,2,1,0:T(2,128)(2,1)}), bf16[128,9,2,128]{3,2,1,0:T(2,128)(2,1)S(1)}, u32[]{:S(2)}, u32[]{:S(2)}) %all-to-all-start.1) | async-done | bytes 589856 | tf_op jit(solution)/shard_map/all_to_all | solution.py:502
  73.7 1.4 %fold.1 = bf16[2304,128]{1,0:T(8,128)(2,1)} custom-call(bf16[2304,128]{1,0:T(8,128)(2,1)S(1)} %bitcast.18), custom_call_target="tpu_custom_call" | custom-call | tf_op jit(solution)/shard_map/fold/pallas_call | solution.py:530
  75.2 7.7 %all-to-all-start.2 = ((bf16[128,9,2,128]{3,2,1,0:T(2,128)(2,1)}), bf16[128,9,2,128]{3,2,1,0:T(2,128)(2,1)S(1)}, u32[]{:S(2)}, u32[]{:S(2)}) async-start(bf16[128,9,2,128]{3,2,1,0:T(2,128)(2,1)} %bitcast.11), calls=%async_computation.2 | async-start | bytes 1179648 | tf_op jit(solution)/shard_map/all_to_all | solution.py:539
  82.9 11.0 %tail.1 = (f32[9,512,512]{2,1,0:T(8,128)}, f32[128,512]{1,0:T(8,128)}) custom-call(bf16[9,256,512]{2,1,0:T(8,128)(2,1)} %get-tuple-element.53.table, bf16[128,512]{1,0:T(8,128)(2,1)} %w_down.3, bf16[9,512,512]{2,1,0:T(8,128)(2,1)} %bitcast.21), custom_call_target="tpu_custom_call" | custom-call | tf_op jit(solution)/shard_map/tail/pallas_call | solution.py:540
  93.9 3.7 %all-to-all-done.2 = bf16[128,9,2,128]{3,2,1,0:T(2,128)(2,1)S(1)} async-done(((bf16[128,9,2,128]{3,2,1,0:T(2,128)(2,1)}), bf16[128,9,2,128]{3,2,1,0:T(2,128)(2,1)S(1)}, u32[]{:S(2)}, u32[]{:S(2)}) %all-to-all-start.2) | async-done | bytes 589856 | tf_op jit(solution)/shard_map/all_to_all | solution.py:539
  97.5 1.0 %finish.1 = (f32[1152,128]{1,0:T(8,128)}, f32[1152,128]{1,0:T(8,128)}) custom-call(bf16[2304,128]{1,0:T(8,128)(2,1)S(1)} %bitcast.19), custom_call_target="tpu_custom_call" | custom-call | tf_op jit(solution)/shard_map/finish/pallas_call | solution.py:557
  (14 shorter events, 0.3 us)
Async XLA Ops:
  1.5 8.0 %collective-permute-start.1 = (bf16[4,48,128]{2,1,0:T(8,128)(2,1)S(1)}, bf16[4,48,128]{2,1,0:T(8,128)(2,1)S(1)}, u32[]{:S(2)}, u32[]{:S(2)}) collective-permute-start(bf16[4,48,128]{2,1,0:T(8,128)(2,1)S(1)} %get-tuple-element.71), channel_id=1, source_target_pairs={{16,32},{32,16},{48,64},{64,48},{80,96},{96,80},{17,33},{33,17},{4... | collective-permute-start | bytes 147464 | tf_op jit(solution)/shard_map/ppermute | solution.py:403
  2.1 8.4 %collective-permute-start = (bf16[4,48,128]{2,1,0:T(8,128)(2,1)S(1)}, bf16[4,48,128]{2,1,0:T(8,128)(2,1)S(1)}, u32[]{:S(2)}, u32[]{:S(2)}) collective-permute-start(bf16[4,48,128]{2,1,0:T(8,128)(2,1)S(1)} %get-tuple-element.72), channel_id=1, source_target_pairs={{0,16},{16,0},{32,48},{48,32},{64,80},{80,64},{96,112},{112,96},{1... | collective-permute-start | bytes 147464 | tf_op jit(solution)/shard_map/ppermute | solution.py:402
  9.4 39.7 %copy-start.1 = (bf16[512,128]{1,0:T(8,128)(2,1)S(1)}, bf16[512,128]{1,0:T(8,128)(2,1)}, u32[]{:S(2)}) copy-start(bf16[512,128]{1,0:T(8,128)(2,1)} %w_up.3) | copy-start | bytes 393220
  10.6 3.9 %collective-permute-start.3 = (bf16[20,2,256]{2,1,0:T(2,128)(2,1)S(1)}, bf16[20,2,256]{2,1,0:T(2,128)(2,1)S(1)}, u32[]{:S(2)}, u32[]{:S(2)}) collective-permute-start(bf16[20,2,256]{2,1,0:T(2,128)(2,1)S(1)} %maximum_maximum_fusion.1), channel_id=1, source_target_pairs={{0,1},{1,2},{2,3},{3,4},{4,5},{5,6},{6,7},{7,8},{8,9},{9,10},{10,1... | collective-permute-start | bytes 61448 | tf_op jit(solution)/shard_map/ppermute | solution.py:419
  13.6 3.6 %collective-permute-start.2 = (bf16[20,2,256]{2,1,0:T(2,128)(2,1)S(1)}, bf16[20,2,256]{2,1,0:T(2,128)(2,1)S(1)}, u32[]{:S(2)}, u32[]{:S(2)}) collective-permute-start(bf16[20,2,256]{2,1,0:T(2,128)(2,1)S(1)} %maximum_maximum_fusion), channel_id=1, source_target_pairs={{1,0},{2,1},{3,2},{4,3},{5,4},{6,5},{7,6},{8,7},{9,8},{10,9},{11,1... | collective-permute-start | bytes 61448 | tf_op jit(solution)/shard_map/ppermute | solution.py:418
  22.3 26.8 %all-to-all-start = ((bf16[128,24,128]{2,1,0:T(8,128)(2,1)}), bf16[128,24,128]{2,1,0:T(8,128)(2,1)S(1)}, u32[]{:S(2)}, u32[]{:S(2)}) async-start(bf16[128,24,128]{2,1,0:T(8,128)(2,1)} %get-tuple-element.34), calls=%async_computation | async-start | bytes 1572864 | tf_op jit(solution)/shard_map/all_to_all | solution.py:472
  49.1 9.9 %copy-start = (bf16[128,24,128]{2,1,0:T(8,128)(2,1)}, bf16[128,24,128]{2,1,0:T(8,128)(2,1)S(1)}, u32[]{:S(2)}) copy-start(bf16[128,24,128]{2,1,0:T(8,128)(2,1)S(1)} %all-to-all-done) | copy-start | bytes 2359300
  54.7 19.0 %all-to-all-start.1 = ((bf16[128,9,2,128]{3,2,1,0:T(2,128)(2,1)}), bf16[128,9,2,128]{3,2,1,0:T(2,128)(2,1)S(1)}, u32[]{:S(2)}, u32[]{:S(2)}) async-start(bf16[128,9,2,128]{3,2,1,0:T(2,128)(2,1)} %bitcast.28), calls=%async_computation.1 | async-start | bytes 1179648 | tf_op jit(solution)/shard_map/all_to_all | solution.py:502
  75.2 22.4 %all-to-all-start.2 = ((bf16[128,9,2,128]{3,2,1,0:T(2,128)(2,1)}), bf16[128,9,2,128]{3,2,1,0:T(2,128)(2,1)S(1)}, u32[]{:S(2)}, u32[]{:S(2)}) async-start(bf16[128,9,2,128]{3,2,1,0:T(2,128)(2,1)} %bitcast.11), calls=%async_computation.2 | async-start | bytes 1179648 | tf_op jit(solution)/shard_map/all_to_all | solution.py:539

commit v3 on v2

--- a/solution.py
+++ b/solution.py
@@ -3,10 +3,13 @@
 from jax import lax
 from jax.experimental import pallas as pl
 from jax.experimental.pallas import tpu as pltpu
+from jax.sharding import Mesh
 from jax.sharding import PartitionSpec as P
 
 POOL = 8
-AXES = ("lat", "lon")
+LON = ("pair", "core")
+PEERS = ("lat", "pair")
+EVERYONE = ("lat", "pair", "core")
 ROWS, COLS, DEPTH = 16, 48, 128
 WIDE = 512
 STRIDE = 64
@@ -15,7 +18,8 @@
 OWN = ROWS * STRIDE
 CROW, CCOL = ROWS // POOL, COLS // POOL
 NLAT, NLON = 8, 16
-COUNT = NLAT * NLON
+COUNT = NLAT * NLON // 2
+HALF = COUNT * 18
 GROW, GCOL = NLAT * CROW, NLON * CCOL
 CELLS = GROW * GCOL
 PACK = 2 * CROW * CCOL
@@ -135,29 +139,41 @@
         copy.wait()
 
 
-def weight_kernel(w_down, w_bot, out):
-    out[0] = mm(w_down[...], w_bot[0]).astype(BF16)
+def weight_kernel(w_down, w_bot_far, out_far, w_bot, out, sems):
+    fetches = [pltpu.make_async_copy(w_bot_far.at[k], w_bot.at[k], sems.at[k]) for k in range(9)]
+    stores = [pltpu.make_async_copy(out.at[k], out_far.at[k], sems.at[9 + k]) for k in range(9)]
+    for fetch in fetches:
+        fetch.start()
+    for k in range(9):
+        fetches[k].wait()
+        out[k] = mm(w_down[...], w_bot[k]).astype(BF16)
+        stores[k].start()
+    for store in stores:
+        store.wait()
 
 
 def third(value):
     return (value * 43) >> 8
 
 
-def source_of(row, col, shift):
+def source_of(row, col, shift, core, first, lats):
     inside = (row >= 0) & (row < GROW)
     col = jnp.where(col < 0, col + GCOL, col)
     col = jnp.where(col >= GCOL, col - GCOL, col)
     group = third(col)
-    device = (row >> 1) * NLON + group
-    return jnp.where(inside, device * PACK + shift + (row & 1) * CCOL + (col - group * CCOL), -1)
+    place = ((row >> 1) - first) * (NLON // 2) + (group >> 1)
+    half = jnp.where((group & 1) == core, 0, lats * (NLON // 2) * PACK)
+    return jnp.where(
+        inside, half + place * PACK + shift + (row & 1) * CCOL + (col - group * CCOL), -1
+    )
 
 
 def second_kernel(
-    pos, every, w_up, w_eff_far, hid_far, slope_far, dm_far, field_far, grad_far,
-    parts_out, merged_out, dact_out,
-    parts, w_eff, hid, slope, dm, field, own_grad, fine_cat, merged_cat, merged_here, dact_here, sems,
+    pos, every, every_far, w_up, w_eff_far, hid_far, slope_far, dm_far, field_far, grad_far,
+    keep_out, give_out, merged_out, dact_out,
+    keep, give, w_eff, hid, slope, dm, field, own_grad, fine_cat, merged_cat, merged_here, dact_here, sems,
 ):
-    lat, lon = pos[0], pos[1]
+    lat, lon, core = pos[0], pos[1], pos[2]
     fetches = [
         pltpu.make_async_copy(a, b, sems.at[k])
         for k, (a, b) in enumerate(
@@ -174,26 +190,33 @@
     stores = [
         pltpu.make_async_copy(merged_here, merged_out, sems.at[6]),
         pltpu.make_async_copy(dact_here, dact_out, sems.at[7]),
-        pltpu.make_async_copy(parts.at[0:1152, :], parts_out.at[0:1152, :], sems.at[8]),
-        pltpu.make_async_copy(parts.at[1152:, :], parts_out.at[1152:, :], sems.at[9]),
+        pltpu.make_async_copy(give, give_out, sems.at[8]),
+        pltpu.make_async_copy(keep, keep_out, sems.at[9]),
     ]
     for fetch in fetches:
         fetch.start()
     own_grad[:, COLS:, :] = jnp.zeros((ROWS, STRIDE - COLS, DEPTH), BF16)
+    lats = 5
+    first = jnp.clip(lat - 2, 0, NLAT - lats)
     spot = lax.broadcasted_iota(jnp.int32, (8 * WIN, 1), 0)
     line, slot = spot >> 4, spot & (WIN - 1)
-    src = source_of(CROW * lat + line - 3, CCOL * lon + slot - 3, 0)
+    src = source_of(CROW * lat + line - 3, CCOL * lon + slot - 3, 0, core, first, lats)
     src = jnp.where(slot < CCOL + 6, src, -1)
     spot = lax.broadcasted_iota(jnp.int32, (6 * WIN, 1), 0)
     line, slot = spot >> 4, spot & (WIN - 1)
-    dsrc = source_of(CROW * lat + line - 2, CCOL * lon + slot - 2, CROW * CCOL)
+    dsrc = source_of(
+        CROW * lat + line - 2, CCOL * lon + slot - 2, CROW * CCOL, core, first, lats
+    )
     dsrc = jnp.where(slot < CCOL + 4, dsrc, -1)
-    reach = 5 * NLON * PACK
-    begin = jnp.clip(lat - 2, 0, NLAT - 5) * (NLON * PACK)
-    near = every[pl.ds(pl.multiple_of(begin, NLON * PACK), reach), :]
-    spots = lax.broadcasted_iota(jnp.int32, (8 * WIN, reach), 1) + begin
+    strip = NLON // 2 * PACK
+    begin = pl.multiple_of(first * strip, strip)
+    reach = lats * strip
+    near = jnp.concatenate(
+        [every[pl.ds(begin, reach), :], every_far[pl.ds(begin, reach), :]], axis=0
+    )
+    spots = lax.broadcasted_iota(jnp.int32, (8 * WIN, 2 * reach), 1)
     pooled = mm((spots == src).astype(F32).astype(BF16), near)
-    spots = lax.broadcasted_iota(jnp.int32, (6 * WIN, reach), 1) + begin
+    spots = lax.broadcasted_iota(jnp.int32, (6 * WIN, 2 * reach), 1)
     dlift = mm((spots == dsrc).astype(F32).astype(BF16), near).astype(BF16)
     shifted = [pooled.astype(BF16)] + [
         pltpu.roll(pooled, 8 * WIN - step, 0).astype(BF16) for step in (1, 2)
@@ -251,38 +274,42 @@
     center = dact_here[2 * STRIDE : 2 * STRIDE + OWN, :]
     own_dact = jnp.where(slot < COLS, center, jnp.zeros_like(center))
     center_grad = own_grad[...].reshape(OWN, DEPTH)
+    zero = core == 0
     for tap in range(3):
+        rows = slice(tap * 384, tap * 384 + 384)
         start = (tap + 1) * STRIDE
-        parts[tap * 384 : tap * 384 + 384, :] = mm(
-            merged_cat[start : start + OWN, :], center_grad, ((0,), (0,))
-        ).astype(BF16)
+        dec = mm(merged_cat[start : start + OWN, :], center_grad, ((0,), (0,))).astype(BF16)
+        start = (tap + 2) * STRIDE
+        enc = mm(fine_cat[start : start + OWN, :], own_dact, ((0,), (0,))).astype(BF16)
+        give[rows, :] = jnp.where(zero, enc, dec)
+        keep[rows, :] = jnp.where(zero, dec, enc)
     stores[2].start()
-    for tap in range(3):
-        start = (tap + 2) * STRIDE
-        parts[1152 + tap * 384 : 1152 + tap * 384 + 384, :] = mm(
-            fine_cat[start : start + OWN, :], own_dact, ((0,), (0,))
-        ).astype(BF16)
     stores[3].start()
     for store in stores:
         store.wait()
 
 
-def third_kernel(merged, dact, w_dec, w_enc, block_out, field_grad, merged_cat, dact_cat):
-    merged_cat[...] = side_by_side(merged[...])
-    dact_cat[...] = side_by_side(dact[...])
-    out = jnp.zeros((OWN, DEPTH), F32)
-    back = jnp.zeros((OWN, DEPTH), F32)
-    for tap in range(3):
-        start = (tap + 1) * STRIDE
-        out = out + mm(merged_cat[start : start + OWN, :], w_dec[tap])
-        back = back + mm(dact_cat[start : start + OWN, :], mirrored(w_enc, tap), ((1,), (1,)))
-    block_out[...] = out.astype(BF16).reshape(ROWS, STRIDE, DEPTH)[:, :COLS, :]
-    field_grad[...] = back.astype(BF16).reshape(ROWS, STRIDE, DEPTH)[:, :COLS, :]
-
-
-def coarse_kernel(every, w_eff, w_up, table, g_up, pooled_cat, dlift, zact, dz):
+def coarse_kernel(
+    pos, w_up, every_out, every_far_out, w_eff_out, table_out, g_up,
+    every, every_far, w_eff, table, pooled_cat, dlift, zact, dz, sems,
+):
+    fetches = [
+        pltpu.make_async_copy(a, b, sems.at[k])
+        for k, (a, b) in enumerate(
+            ((every_out, every), (every_far_out, every_far), (w_eff_out, w_eff))
+        )
+    ]
+    stores = [
+        pltpu.make_async_copy(
+            table.at[3 * k : 3 * k + 3], table_out.at[3 * k : 3 * k + 3], sems.at[3 + k]
+        )
+        for k in range(3)
+    ]
+    for fetch in fetches:
+        fetch.start()
     line = 2 * GCOL
-    block = NLON * PACK
+    core = pos[2]
+    strip = NLON // 2 * PACK
     spot = lax.broadcasted_iota(jnp.int32, (4 * line, 1), 0)
     kind = (spot >= line).astype(jnp.int32) + (spot >= 2 * line).astype(jnp.int32)
     kind = kind + (spot >= 3 * line).astype(jnp.int32)
@@ -291,16 +318,24 @@
     col = within - row * GCOL
     col = jnp.where(kind < 3, col + kind - 1, col)
     shift = jnp.where(kind < 3, 0, CROW * CCOL)
-    src = source_of(row, col, shift)
-    spots = lax.broadcasted_iota(jnp.int32, (4 * line, block), 1)
+    src = source_of(row, col, shift, core, 0, 1)
+    spots = lax.broadcasted_iota(jnp.int32, (4 * line, 2 * strip), 1)
     order = (spots == src).astype(F32).astype(BF16)
     edge = jnp.zeros((GCOL, 3 * DEPTH), BF16)
     pooled_cat[0:GCOL, :] = edge
     pooled_cat[(GROW + 1) * GCOL :, :] = edge
+    fetches[0].wait()
+    fetches[1].wait()
     for pair in range(NLAT // 2):
         both = jnp.concatenate(
-            [every[(2 * pair + k) * block : (2 * pair + k + 1) * block, :] for k in (0, 1)],
-            axis=1,
+            [
+                jnp.concatenate(
+                    [part[(2 * pair + k) * strip : (2 * pair + k + 1) * strip, :] for k in (0, 1)],
+                    axis=1,
+                )
+                for part in (every, every_far)
+            ],
+            axis=0,
         )
         moved = mm(order, both).astype(BF16)
         for k in (0, 1):
@@ -312,58 +347,115 @@
                     b * line : (b + 1) * line, lanes
                 ]
             dlift[lat * line : (lat + 1) * line, :] = moved[3 * line :, lanes]
-    for part in range(NLAT):
-        base = part * line
-        zpre = jnp.zeros((line, WIDE), F32)
-        for tap in range(3):
-            at = base + tap * GCOL
-            zpre = zpre + mm(pooled_cat[at : at + line, :], w_eff[tap * 384 : tap * 384 + 384, :])
+    fetches[2].wait()
+    rows = 384
+    for part in range(CELLS // rows):
+        base = part * rows
+        spread = jnp.concatenate(
+            [pooled_cat[base + tap * GCOL : base + tap * GCOL + rows, :] for tap in range(3)], axis=1
+        )
+        zpre = mm(spread, w_eff[...])
         sig = jax.nn.sigmoid(zpre)
-        zact[base : base + line, :] = (zpre * sig).astype(BF16)
-        up = mm(dlift[base : base + line, :], w_up[...], ((1,), (1,)))
-        dz[base : base + line, :] = (up * (sig * (1.0 + zpre * (1.0 - sig)))).astype(BF16)
-    g_up[...] = mm(zact[...], dlift[...], ((0,), (0,)))
+        zact[base : base + rows, :] = (zpre * sig).astype(BF16)
+        up = mm(dlift[base : base + rows, :], w_up[...], ((1,), (1,)))
+        dz[GCOL + base : GCOL + base + rows, :] = (up * (sig * (1.0 + zpre * (1.0 - sig)))).astype(BF16)
+    blank = jnp.zeros((GCOL, WIDE), BF16)
+    dz[0:GCOL, :] = blank
+    dz[GCOL + CELLS :, :] = blank
+    lying = pooled_cat[GCOL : GCOL + CELLS, :].T
     for tap in range(3):
-        at = tap * GCOL
-        corr = mm(pooled_cat[at : at + CELLS, :], dz[...], ((0,), (0,)))
-        high, low = split_two(corr)
-        for b in range(3):
-            lanes = slice(b * DEPTH, (b + 1) * DEPTH)
-            table[tap * 3 + b, 0:DEPTH, :] = high[lanes]
-            table[tap * 3 + b, DEPTH:, :] = low[lanes]
+        at = (2 - tap) * GCOL
+        corr = mm(lying, dz[at : at + CELLS, :]).astype(BF16)
+        table[3 * tap : 3 * tap + 3] = corr.reshape(3, DEPTH, WIDE)
+        stores[tap].start()
+    g_up[...] = mm(dlift[...].T, zact[...]).T
+    for store in stores:
+        store.wait()
 
 
 def remainder(value):
     return value - 18 * ((value * 3641) >> 16)
 
 
+def add_kernel(got, keep_far, out, keep, sems):
+    fetch = pltpu.make_async_copy(keep_far, keep, sems.at[0])
+    fetch.start()
+    fetch.wait()
+    out[...] = (keep[...].astype(F32) + got[...].astype(F32)).astype(BF16)
+
+
 def fold_kernel(spread, out):
-    full = COUNT * 18
-    slot = remainder(lax.broadcasted_iota(jnp.int32, (32, full), 1))
-    pick = slot == lax.broadcasted_iota(jnp.int32, (32, full), 0)
+    slot = remainder(lax.broadcasted_iota(jnp.int32, (32, HALF), 1))
+    pick = slot == lax.broadcasted_iota(jnp.int32, (32, HALF), 0)
     total = mm(pick.astype(F32).astype(BF16), spread[...]).astype(BF16)
-    slot = remainder(lax.broadcasted_iota(jnp.int32, (full, 1), 0))
-    copy = lax.broadcasted_iota(jnp.int32, (full, 32), 1) == slot
+    slot = remainder(lax.broadcasted_iota(jnp.int32, (2 * HALF, 1), 0))
+    copy = lax.broadcasted_iota(jnp.int32, (2 * HALF, 32), 1) == slot
     out[...] = mm(copy.astype(F32).astype(BF16), total).astype(BF16)
 
 
 def finish_kernel(whole, g_dec, g_enc):
-    g_dec[...] = whole[:1152].astype(F32)
-    g_enc[...] = whole[1152:].astype(F32)
-
-
-def tail_kernel(table, w_down, w_bot, g_bot, g_down):
-    step = pl.program_id(0)
-
-    @pl.when(step == 0)
-    def _():
-        g_down[...] = jnp.zeros((DEPTH, WIDE), F32)
-
-    pair = table[0]
-    twice = jnp.concatenate([w_down[...], w_down[...]], axis=0)
-    g_bot[0] = mm(twice, pair, ((0,), (0,)))
-    back = mm(pair, w_bot[0], ((1,), (1,)))
-    g_down[...] += back[:DEPTH] + back[DEPTH:]
+    row = lax.broadcasted_iota(jnp.int32, (144, 1), 0)
+    half = (row >= 72).astype(jnp.int32)
+    rest = row - 72 * half
+    step = sum((rest >= 18 * k).astype(jnp.int32) for k in (1, 2, 3))
+    src = rest + 18 * step + 18 * half
+    order = (lax.broadcasted_iota(jnp.int32, (144, 144), 1) == src).astype(F32).astype(BF16)
+    for block in range(16):
+        rows = mm(order, whole[144 * block : 144 * block + 144, :])
+        g_dec[72 * block : 72 * block + 72, :] = rows[:72]
+        g_enc[72 * block : 72 * block + 72, :] = rows[72:]
+
+
+def tail_kernel(
+    w_down, table_far, merged_far, dact_far, w_dec_far, w_enc_far, w_bot_far,
+    g_bot_far, block_far, back_far, g_down,
+    table, merged, dact, w_dec, w_enc, w_bot, g_bot, merged_cat, dact_cat, block, back, sems,
+):
+    fetches = [
+        pltpu.make_async_copy(a, b, sems.at[18 + k])
+        for k, (a, b) in enumerate(
+            (
+                (table_far, table),
+                (merged_far, merged),
+                (dact_far, dact),
+                (w_dec_far, w_dec),
+                (w_enc_far, w_enc),
+            )
+        )
+    ]
+    loads = [pltpu.make_async_copy(w_bot_far.at[k], w_bot.at[k], sems.at[k]) for k in range(9)]
+    stores = [pltpu.make_async_copy(g_bot.at[k], g_bot_far.at[k], sems.at[9 + k]) for k in range(9)]
+    stores.append(pltpu.make_async_copy(block.at[:, 0:COLS, :], block_far, sems.at[23]))
+    stores.append(pltpu.make_async_copy(back.at[:, 0:COLS, :], back_far, sems.at[24]))
+    for fetch in fetches:
+        fetch.start()
+    for load in loads:
+        load.start()
+    fetches[0].wait()
+    for k in range(9):
+        g_bot[k] = mm(w_down[...], table[k], ((0,), (0,)))
+        stores[k].start()
+    for fetch in fetches[1:]:
+        fetch.wait()
+    merged_cat[...] = side_by_side(merged[...])
+    dact_cat[...] = side_by_side(dact[...])
+    fore = jnp.zeros((OWN, DEPTH), F32)
+    aft = jnp.zeros((OWN, DEPTH), F32)
+    for tap in range(3):
+        start = (tap + 1) * STRIDE
+        fore = fore + mm(merged_cat[start : start + OWN, :], w_dec[tap])
+        aft = aft + mm(dact_cat[start : start + OWN, :], mirrored(w_enc, tap), ((1,), (1,)))
+    block[...] = fore.astype(BF16).reshape(ROWS, STRIDE, DEPTH)
+    stores[9].start()
+    back[...] = aft.astype(BF16).reshape(ROWS, STRIDE, DEPTH)
+    stores[10].start()
+    total = jnp.zeros((DEPTH, WIDE), F32)
+    for k in range(9):
+        loads[k].wait()
+        total = total + mm(table[k], w_bot[k], ((1,), (1,)))
+    g_down[...] = total
+    for store in stores:
+        store.wait()
 
 
 def vmem():
@@ -391,7 +483,9 @@
 
 
 def body(fine, w_enc, w_down, w_bot, w_up, w_dec, grad):
-    pos = jnp.stack([lax.axis_index("lat"), lax.axis_index("lon")]).astype(jnp.int32)
+    pos = jnp.stack([lax.axis_index("lat"), lax.axis_index(LON), lax.axis_index("core")])
+    pos = pos.astype(jnp.int32)
+    swap = [(0, 1), (1, 0)]
     inner = [(i, i ^ 1) for i in range(NLAT)]
     outer = [(i, ((i + 1) ^ 1) - 1) for i in range(1, NLAT - 1)]
     even = lax.axis_index("lat") % 2 == 0
@@ -415,8 +509,8 @@
 
     first = edge(slice(0, 2))
     last = edge(slice(COLS - 2, COLS))
-    high = lax.ppermute(first, "lon", left)
-    low = lax.ppermute(last, "lon", right)
+    high = lax.ppermute(first, LON, left)
+    low = lax.ppermute(last, LON, right)
     strip = jnp.concatenate(
         [
             jnp.pad(high, ((1, 0), (0, 0), (0, 0))),
@@ -425,18 +519,6 @@
         ],
         axis=1,
     )
-    w_eff = pl.pallas_call(
-        weight_kernel,
-        grid=(9,),
-        in_specs=[
-            pl.BlockSpec((DEPTH, WIDE), lambda i: (0, 0)),
-            pl.BlockSpec((1, WIDE, WIDE), lambda i: (i, 0, 0)),
-        ],
-        out_specs=pl.BlockSpec((1, DEPTH, WIDE), lambda i: (i, 0, 0)),
-        out_shape=shape((9, DEPTH, WIDE), BF16),
-        name="weights",
-        compiler_params=grant(56),
-    )(w_down, w_bot.reshape(9, WIDE, WIDE)).reshape(9 * DEPTH, WIDE)
     w_enc_f = w_enc.reshape(3, 3 * DEPTH, DEPTH)
     w_dec_f = w_dec.reshape(3, 3 * DEPTH, DEPTH)
     pack, hid, slope, dm, field = pl.pallas_call(
@@ -469,18 +551,36 @@
         pos, got_inner, got_outer, strip,
         *(held(x) for x in (fine, grad, w_enc_f, w_dec.reshape(9, DEPTH, DEPTH))),
     )
-    every = lax.all_to_all(pack, AXES, 0, 0).reshape(COUNT * PACK, DEPTH)
-    parts, merged, dact = pl.pallas_call(
+    pack, early = lax.optimization_barrier((pack, w_down))
+    every = lax.all_to_all(pack, PEERS, 0, 0).reshape(COUNT * PACK, DEPTH)
+    w_eff = pl.pallas_call(
+        weight_kernel,
+        in_specs=[vmem(), far()],
+        out_specs=far(),
+        out_shape=pltpu.HBM((9, DEPTH, WIDE), BF16),
+        scratch_shapes=[
+            pltpu.VMEM((9, WIDE, WIDE), BF16),
+            pltpu.VMEM((9, DEPTH, WIDE), BF16),
+            pltpu.SemaphoreType.DMA((18,)),
+        ],
+        name="weights",
+        compiler_params=grant(56),
+    )(early, held(w_bot.reshape(9, WIDE, WIDE))).reshape(9 * DEPTH, WIDE)
+    every, w_eff = lax.optimization_barrier((every, w_eff))
+    every_far = lax.ppermute(every, "core", swap)
+    keep, give, merged, dact = pl.pallas_call(
         second_kernel,
-        in_specs=[smem(), vmem(), vmem()] + [far()] * 6,
-        out_specs=[far()] * 3,
+        in_specs=[smem(), vmem(), vmem(), vmem()] + [far()] * 6,
+        out_specs=[far()] * 4,
         out_shape=[
-            pltpu.HBM((2304, DEPTH), BF16),
+            pltpu.HBM((HALF, DEPTH), BF16),
+            pltpu.HBM((HALF, DEPTH), BF16),
             pltpu.HBM((RIM, DEPTH), BF16),
             pltpu.HBM((RIM, DEPTH), BF16),
         ],
         scratch_shapes=[
-            pltpu.VMEM((2304, DEPTH), BF16),
+            pltpu.VMEM((HALF, DEPTH), BF16),
+            pltpu.VMEM((HALF, DEPTH), BF16),
             pltpu.VMEM((9 * DEPTH, WIDE), BF16),
             pltpu.VMEM((RIM, DEPTH), BF16),
             pltpu.VMEM((RIM, DEPTH), F32),
@@ -495,83 +595,109 @@
         ],
         name="second",
         compiler_params=grant(30),
-    )(pos, every, w_up, *(held(x) for x in (w_eff, hid, slope, dm, field, grad)))
-    parts, later, merged, dact = lax.optimization_barrier(
-        (parts, every, merged, dact)
-    )
-    spread = lax.all_to_all(parts.reshape(COUNT, 9, 2, DEPTH), AXES, 0, 0)
+    )(pos, every, every_far, w_up, *(held(x) for x in (w_eff, hid, slope, dm, field, grad)))
+    keep, give, every, every_far, merged, dact = lax.optimization_barrier(
+        (keep, give, every, every_far, merged, dact)
+    )
+    got = lax.ppermute(give, "core", swap)
+    half = pl.pallas_call(
+        add_kernel,
+        in_specs=[vmem(), far()],
+        out_specs=vmem(),
+        out_shape=shape((HALF, DEPTH), BF16),
+        scratch_shapes=[pltpu.VMEM((HALF, DEPTH), BF16), pltpu.SemaphoreType.DMA((1,))],
+        name="add",
+        compiler_params=grant(6),
+    )(got, held(keep))
+    half, every, every_far = lax.optimization_barrier((half, every, every_far))
+    spread = lax.all_to_all(half.reshape(COUNT, 9, 2, DEPTH), PEERS, 0, 0)
     table, g_up = pl.pallas_call(
         coarse_kernel,
-        in_specs=[vmem()] * 3,
-        out_specs=[vmem()] * 2,
-        out_shape=[
-            shape((9, 2 * DEPTH, WIDE), BF16),
-            shape((WIDE, DEPTH), F32),
-        ],
+        in_specs=[smem(), vmem(), far(), far(), far()],
+        out_specs=[far(), vmem()],
+        out_shape=[pltpu.HBM((9, DEPTH, WIDE), BF16), shape((WIDE, DEPTH), F32)],
         scratch_shapes=[
+            pltpu.VMEM((COUNT * PACK, DEPTH), BF16),
+            pltpu.VMEM((COUNT * PACK, DEPTH), BF16),
+            pltpu.VMEM((9 * DEPTH, WIDE), BF16),
+            pltpu.VMEM((9, DEPTH, WIDE), BF16),
             pltpu.VMEM(((GROW + 2) * GCOL, 3 * DEPTH), BF16),
             pltpu.VMEM((CELLS, DEPTH), BF16),
             pltpu.VMEM((CELLS, WIDE), BF16),
-            pltpu.VMEM((CELLS, WIDE), BF16),
+            pltpu.VMEM((CELLS + 2 * GCOL, WIDE), BF16),
+            pltpu.SemaphoreType.DMA((6,)),
         ],
         name="coarse",
         compiler_params=grant(56),
-    )(later, w_eff, w_up)
-    block_out, field_grad = pl.pallas_call(
-        third_kernel,
-        in_specs=[vmem()] * 4,
-        out_specs=[vmem()] * 2,
-        out_shape=[shape((ROWS, COLS, DEPTH), BF16)] * 2,
-        scratch_shapes=[pltpu.VMEM((RIM, 3 * DEPTH), BF16)] * 2,
-        name="third",
-        compiler_params=grant(56),
-    )(merged, dact, w_dec_f, w_enc.reshape(9, DEPTH, DEPTH))
-    spread, table, block_out = lax.optimization_barrier((spread, table, block_out))
+    )(pos, w_up, held(every), held(every_far), held(w_eff))
+    spread, table = lax.optimization_barrier((spread, table))
     total = pl.pallas_call(
         fold_kernel,
         in_specs=[vmem()],
         out_specs=vmem(),
-        out_shape=pltpu.VMEM((2304, DEPTH), BF16),
+        out_shape=pltpu.VMEM((2 * HALF, DEPTH), BF16),
         name="fold",
         compiler_params=grant(8),
-    )(spread.reshape(2304, DEPTH))
-    total, table = lax.optimization_barrier((total, table))
-    whole = lax.all_to_all(total.reshape(COUNT, 9, 2, DEPTH), AXES, 0, 0)
-    g_bot, g_down = pl.pallas_call(
+    )(spread.reshape(HALF, DEPTH))
+    total, table, merged, dact = lax.optimization_barrier((total, table, merged, dact))
+    whole = lax.all_to_all(total.reshape(2 * COUNT, 9, 2, DEPTH), EVERYONE, 0, 0)
+    g_bot, block_out, field_grad, g_down = pl.pallas_call(
         tail_kernel,
-        grid=(9,),
-        in_specs=[
-            pl.BlockSpec((1, 2 * DEPTH, WIDE), lambda i: (i, 0, 0)),
-            pl.BlockSpec((DEPTH, WIDE), lambda i: (0, 0)),
-            pl.BlockSpec((1, WIDE, WIDE), lambda i: (i, 0, 0)),
-        ],
-        out_specs=[
-            pl.BlockSpec((1, WIDE, WIDE), lambda i: (i, 0, 0)),
-            pl.BlockSpec((DEPTH, WIDE), lambda i: (0, 0)),
-        ],
-        out_shape=[shape((9, WIDE, WIDE), F32), shape((DEPTH, WIDE), F32)],
+        in_specs=[vmem()] + [far()] * 6,
+        out_specs=[far()] * 3 + [vmem()],
+        out_shape=[
+            pltpu.HBM((9, WIDE, WIDE), F32),
+            pltpu.HBM((ROWS, COLS, DEPTH), BF16),
+            pltpu.HBM((ROWS, COLS, DEPTH), BF16),
+            shape((DEPTH, WIDE), F32),
+        ],
+        scratch_shapes=[
+            pltpu.VMEM((9, DEPTH, WIDE), BF16),
+            pltpu.VMEM((RIM, DEPTH), BF16),
+            pltpu.VMEM((RIM, DEPTH), BF16),
+            pltpu.VMEM((3, 3 * DEPTH, DEPTH), BF16),
+            pltpu.VMEM((9, DEPTH, DEPTH), BF16),
+            pltpu.VMEM((9, WIDE, WIDE), BF16),
+            pltpu.VMEM((9, WIDE, WIDE), F32),
+            pltpu.VMEM((RIM, 3 * DEPTH), BF16),
+            pltpu.VMEM((RIM, 3 * DEPTH), BF16),
+            pltpu.VMEM((ROWS, STRIDE, DEPTH), BF16),
+            pltpu.VMEM((ROWS, STRIDE, DEPTH), BF16),
+            pltpu.SemaphoreType.DMA((25,)),
+        ],
         name="tail",
         compiler_params=grant(56),
-    )(table, w_down, w_bot.reshape(9, WIDE, WIDE))
-    whole, g_bot = lax.optimization_barrier((whole, g_bot))
+    )(
+        w_down,
+        *(
+            held(x)
+            for x in (
+                table, merged, dact, w_dec_f,
+                w_enc.reshape(9, DEPTH, DEPTH), w_bot.reshape(9, WIDE, WIDE),
+            )
+        ),
+    )
+    whole, g_bot, block_out = lax.optimization_barrier((whole, g_bot, block_out))
     g_dec, g_enc = pl.pallas_call(
         finish_kernel,
         in_specs=[vmem()],
         out_specs=[vmem()] * 2,
-        out_shape=[shape((1152, DEPTH), F32)] * 2,
+        out_shape=[shape((HALF, DEPTH), F32)] * 2,
         name="finish",
         compiler_params=grant(6),
-    )(whole.reshape(2304, DEPTH))
+    )(whole.reshape(2 * HALF, DEPTH))
     g_dec = g_dec.reshape(3, 3, DEPTH, DEPTH)
     g_enc = g_enc.reshape(3, 3, DEPTH, DEPTH)
     return (block_out, field_grad, g_enc, g_down, g_bot.reshape(3, 3, WIDE, WIDE), g_up, g_dec)
 
 
 def solution(mesh):
+    split = Mesh(mesh.devices.reshape(NLAT, NLON // 2, 2), ("lat",) + LON)
+    tile = P("lat", LON, None)
     return jax.shard_map(
         body,
-        mesh=mesh,
-        in_specs=(P("lat", "lon", None), P(), P(), P(), P(), P(), P("lat", "lon", None)),
-        out_specs=(P("lat", "lon", None), P("lat", "lon", None), P(), P(), P(), P(), P()),
+        mesh=split,
+        in_specs=(tile, P(), P(), P(), P(), P(), tile),
+        out_specs=(tile, tile, P(), P(), P(), P(), P()),
         check_vma=False,
     )

time: 99.4 us -> 98.4 us (0.990)
  Pallas kernels: 44.1 us -> 37.6 us
  starting transfers between devices: 32.3 us -> 36.3 us
  waiting for transfers between devices: 19.4 us -> 21.2 us
    pallas_call x5, Pallas kernels: 36.6 us -> 29.9 us  [the longest x1 9.38 us: body(): pl.pallas_call(coarse_kernel, in_specs=[smem(), vmem(), far(), far(), far...]
    all_to_all x3, starting transfers between devices: 22.1 us -> 25.2 us  [the longest x1 11.2 us: body(): every = lax.all_to_all(pack, PEERS, 0, 0).reshape(COUNT * PACK, DEPTH)]
    ppermute x2 -> x4, waiting for transfers between devices: 3.33 us -> 6.09 us  [the longest x1 2.69 us: body(): high = lax.ppermute(first, LON, left)]
    all_to_all x3, waiting for transfers between devices: 15 us -> 14 us  [the longest x1 6.97 us: body(): every = lax.all_to_all(pack, PEERS, 0, 0).reshape(COUNT * PACK, DEPTH)]
    ppermute x2 -> x4, starting transfers between devices: 3.06 us -> 3.92 us  [the longest x1 2.99 us: body(): low = lax.ppermute(last, LON, right)]
  transfers between devices with their start and end apart: 7 -> 9, of which waited for: 6 -> 8; matrix products, arithmetic and copies ran while one was open for 1% -> 1% of each run, Pallas kernels for 31% -> 23%
where the time goes in v3:
time: 98.4 us; the launch traced here: 97.9 us
  Pallas kernels  37.6 us (38%)
  starting transfers between devices  36.3 us (37%)
  waiting for transfers between devices  21.2 us (22%)
  local copies, waits for them, and re-layouts  1.78 us (2%)
    all_to_all x1, starting transfers between devices, body(): every = lax.all_to_all(pack, PEERS, 0, 0).reshape(COUNT * PACK, DEPTH)  11.2 us
    pallas_call x1, Pallas kernels, body(): pl.pallas_call(coarse_kernel, in_specs=[smem(), vmem(), far(), far(), far...  9.38 us
    all_to_all x1, starting transfers between devices, body(): lax.all_to_all(total.reshape(2 * COUNT, 9, 2, DEPTH), EVERYONE, 0, 0)  9.11 us
    pallas_call x1, Pallas kernels, body(): pl.pallas_call(tail_kernel, in_specs=[vmem()] + [far()] * 6, out_specs=[f...  7.89 us
    all_to_all x1, waiting for transfers between devices, body(): every = lax.all_to_all(pack, PEERS, 0, 0).reshape(COUNT * PACK, DEPTH)  6.97 us
    all_to_all x1, waiting for transfers between devices, body(): lax.all_to_all(total.reshape(2 * COUNT, 9, 2, DEPTH), EVERYONE, 0, 0)  6.74 us
    ppermute x1, starting transfers between devices, body(): got_inner = lax.ppermute(jnp.where(even, under, over), 'lat', inner)  6.47 us
    pallas_call x1, Pallas kernels, body(): pl.pallas_call(second_kernel, in_specs=[smem(), vmem(), vmem(), vmem()] +...  5.99 us
  transfers between devices with their start and end apart: 9, of which 8 were waited for; matrix products, arithmetic and copies ran while one was open for 1% of the time, Pallas kernels for 23%

profile of v3, /device:TPU:1, one launch (start us, length us, event | category | flops | bytes accessed | tf_op | source)
XLA Modules:
  0.0 97.9 jit_solution(13882972146426410712)
XLA Ops:
  0.7 0.8 fusion.6
  1.5 0.7 collective-permute-start.1
  2.2 6.5 %collective-permute-start = (bf16[4,48,128]{2,1,0:T(8,128)(2,1)S(1)}, bf16[4,48,128]{2,1,0:T(8,128)(2,1)S(1)}, u32[]{:S(2)}, u32[]{:S(2)}) collective-permute-start(bf16[4,48,128]{2,1,0:T(8,128)(2,1)S(1)} %get-tuple-element.96), channel_id=1, source_target_pairs={{0,16},{16,0},{32,48},{48,32},{64,80},{80,64},{96,112},{112,96},{1... | collective-permute-start | bytes 147464 | tf_op jit(solution)/shard_map/ppermute | solution.py:496
  8.6 0.8 fusion.4
  9.5 1.0 %collective-permute-done.got_inner = bf16[4,48,128]{2,1,0:T(8,128)(2,1)S(1)} collective-permute-done((bf16[4,48,128]{2,1,0:T(8,128)(2,1)S(1)}, bf16[4,48,128]{2,1,0:T(8,128)(2,1)S(1)}, u32[]{:S(2)}, u32[]{:S(2)}) %collective-permute-start) | collective-permute-done | bytes 49184 | tf_op jit(solution)/shard_map/ppermute | solution.py:496
  10.6 3.0 %collective-permute-start.3 = (bf16[20,2,256]{2,1,0:T(2,128)(2,1)S(1)}, bf16[20,2,256]{2,1,0:T(2,128)(2,1)S(1)}, u32[]{:S(2)}, u32[]{:S(2)}) collective-permute-start(bf16[20,2,256]{2,1,0:T(2,128)(2,1)S(1)} %maximum_maximum_fusion.1), channel_id=1, source_target_pairs={{0,1},{1,2},{2,3},{3,4},{4,5},{5,6},{6,7},{7,8},{8,9},{9,10},{10,1... | collective-permute-start | bytes 61448 | tf_op jit(solution)/shard_map/ppermute | solution.py:513
  13.9 0.6 collective-permute-done.3
  14.5 2.7 %collective-permute-done.2 = bf16[20,2,256]{2,1,0:T(2,128)(2,1)S(1)} collective-permute-done((bf16[20,2,256]{2,1,0:T(2,128)(2,1)S(1)}, bf16[20,2,256]{2,1,0:T(2,128)(2,1)S(1)}, u32[]{:S(2)}, u32[]{:S(2)}) %collective-permute-start.2) | collective-permute-done | bytes 20512 | tf_op jit(solution)/shard_map/ppermute | solution.py:512
  17.3 4.9 %first.1 = (bf16[64,24,128]{2,1,0:T(8,128)(2,1)}, bf16[1216,128]{1,0:T(8,128)(2,1)}, f32[1216,128]{1,0:T(8,128)}, f32[1216,128]{1,0:T(8,128)}, bf16[21,64,128]{2,1,0:T(8,128)(2,1)}) custom-call(s32[3]{0:T(128)S(1)} %pad_add_fusion.pos, bf16[4,48,128]{2,1,0:T(8,128)(2,1)S(1)} %collective-permute-done.got_inner, ...), custom_call_target="tpu_custom_call" | custom-call | tf_op jit(solution)/shard_map/first/pallas_call | solution.py:524
  22.2 11.2 %all-to-all-start = ((bf16[64,24,128]{2,1,0:T(8,128)(2,1)}), bf16[64,24,128]{2,1,0:T(8,128)(2,1)S(1)}, u32[]{:S(2)}, u32[]{:S(2)}) async-start(bf16[64,24,128]{2,1,0:T(8,128)(2,1)} %get-tuple-element.47), calls=%async_computation | async-start | bytes 786432 | tf_op jit(solution)/shard_map/all_to_all | solution.py:555
  33.4 4.9 %weights.1 = bf16[9,128,512]{2,1,0:T(8,128)(2,1)} custom-call(bf16[128,512]{1,0:T(8,128)(2,1)} %w_down.2, bf16[9,512,512]{2,1,0:T(8,128)(2,1)} %bitcast.22), custom_call_target="tpu_custom_call" | custom-call | tf_op jit(solution)/shard_map/weights/pallas_call | solution.py:556
  38.3 7.0 %all-to-all-done = bf16[64,24,128]{2,1,0:T(8,128)(2,1)S(1)} async-done(((bf16[64,24,128]{2,1,0:T(8,128)(2,1)}), bf16[64,24,128]{2,1,0:T(8,128)(2,1)S(1)}, u32[]{:S(2)}, u32[]{:S(2)}) %all-to-all-start) | async-done | bytes 393248 | tf_op jit(solution)/shard_map/all_to_all | solution.py:555
  45.7 1.3 %collective-permute-done.4.every_far.every_far_out = bf16[1536,128]{1,0:T(8,128)(2,1)S(1)} collective-permute-done((bf16[1536,128]{1,0:T(8,128)(2,1)S(1)}, bf16[1536,128]{1,0:T(8,128)(2,1)S(1)}, u32[]{:S(2)}, u32[]{:S(2)}) %collective-permute-start.4) | collective-permute-done | bytes 393248 | tf_op jit(solution)/shard_map/ppermute | solution.py:570
  47.0 6.0 %second.1 = (bf16[1152,128]{1,0:T(8,128)(2,1)}, bf16[1152,128]{1,0:T(8,128)(2,1)}, bf16[1216,128]{1,0:T(8,128)(2,1)}, bf16[1216,128]{1,0:T(8,128)(2,1)}) custom-call(s32[3]{0:T(128)S(1)} %pad_add_fusion.pos, bf16[1536,128]{1,0:T(8,128)(2,1)S(1)} %bitcast.18, bf16[1536,128]{1,0:T(8,128)(2,1)S(1)} %collective-permute-done.4.every_far.every_far_out, ...), custom_call_target="tpu_custom_call" | custom-call | tf_op jit(solution)/shard_map/second/pallas_call | solution.py:571
  53.0 0.5 collective-permute-start.5
  53.5 1.4 %collective-permute-done.5.got = bf16[1152,128]{1,0:T(8,128)(2,1)S(1)} collective-permute-done((bf16[1152,128]{1,0:T(8,128)(2,1)}, bf16[1152,128]{1,0:T(8,128)(2,1)S(1)}, u32[]{:S(2)}, u32[]{:S(2)}) %collective-permute-start.5) | collective-permute-done | bytes 294944 | tf_op jit(solution)/shard_map/ppermute | solution.py:602
  54.9 1.7 %add.18 = bf16[1152,128]{1,0:T(8,128)(2,1)} custom-call(bf16[1152,128]{1,0:T(8,128)(2,1)S(1)} %collective-permute-done.5.got, bf16[1152,128]{1,0:T(8,128)(2,1)} %get-tuple-element.60.keep_far), custom_call_target="tpu_custom_call" | custom-call | tf_op jit(solution)/shard_map/add/pallas_call | solution.py:603
  56.7 4.9 %all-to-all-start.1 = ((bf16[64,9,2,128]{3,2,1,0:T(2,128)(2,1)}), bf16[64,9,2,128]{3,2,1,0:T(2,128)(2,1)S(1)}, u32[]{:S(2)}, u32[]{:S(2)}) async-start(bf16[64,9,2,128]{3,2,1,0:T(2,128)(2,1)} %bitcast.8), calls=%async_computation.1 | async-start | bytes 589824 | tf_op jit(solution)/shard_map/all_to_all | solution.py:613
  61.6 9.4 %coarse.1 = (bf16[9,128,512]{2,1,0:T(8,128)(2,1)}, f32[512,128]{1,0:T(8,128)}) custom-call(s32[3]{0:T(128)} %copy-done.3, bf16[512,128]{1,0:T(8,128)(2,1)} %w_up.3, bf16[1536,128]{1,0:T(8,128)(2,1)} %bitcast.19, bf16[1536,128]{1,0:T(8,128)(2,1)} %copy-done.1, bf16[1152,512]{1,0:T(8,128)(2,1)} %bitcast.25), custom_call_target="tpu_custom_call" | custom-call | tf_op jit(solution)/shard_map/coarse/pallas_call | solution.py:614
  71.3 1.4 %fold.1 = bf16[2304,128]{1,0:T(8,128)(2,1)} custom-call(bf16[1152,128]{1,0:T(8,128)(2,1)S(1)} %bitcast.21), custom_call_target="tpu_custom_call" | custom-call | tf_op jit(solution)/shard_map/fold/pallas_call | solution.py:634
  72.7 9.1 %all-to-all-start.2 = ((bf16[128,9,2,128]{3,2,1,0:T(2,128)(2,1)}), bf16[128,9,2,128]{3,2,1,0:T(2,128)(2,1)S(1)}, u32[]{:S(2)}, u32[]{:S(2)}) async-start(bf16[128,9,2,128]{3,2,1,0:T(2,128)(2,1)} %bitcast.10), calls=%async_computation.2 | async-start | bytes 1179648 | tf_op jit(solution)/shard_map/all_to_all | solution.py:643
  81.8 7.9 %tail.1 = (f32[9,512,512]{2,1,0:T(8,128)}, bf16[16,48,128]{2,1,0:T(8,128)(2,1)}, bf16[16,48,128]{2,1,0:T(8,128)(2,1)}, f32[128,512]{1,0:T(8,128)}) custom-call(bf16[128,512]{1,0:T(8,128)(2,1)} %w_down.2, bf16[9,128,512]{2,1,0:T(8,128)(2,1)} %get-tuple-element.72.table_far, bf16[1216,128]{1,0:T(8,128)(2,1)} %get-tuple-element.73.merged_far, ...), custom_call_target="tpu_custom_call" | custom-call | tf_op jit(solution)/shard_map/tail/pallas_call | solution.py:644
  89.7 6.7 %all-to-all-done.2 = bf16[128,9,2,128]{3,2,1,0:T(2,128)(2,1)S(1)} async-done(((bf16[128,9,2,128]{3,2,1,0:T(2,128)(2,1)}), bf16[128,9,2,128]{3,2,1,0:T(2,128)(2,1)S(1)}, u32[]{:S(2)}, u32[]{:S(2)}) %all-to-all-start.2) | async-done | bytes 589856 | tf_op jit(solution)/shard_map/all_to_all | solution.py:643
  96.5 1.4 %finish.1 = (f32[1152,128]{1,0:T(8,128)}, f32[1152,128]{1,0:T(8,128)}) custom-call(bf16[2304,128]{1,0:T(8,128)(2,1)S(1)} %bitcast.20), custom_call_target="tpu_custom_call" | custom-call | tf_op jit(solution)/shard_map/finish/pallas_call | solution.py:681
  (22 shorter events, 1.1 us)
Async XLA Ops:
  0.6 46.4 %copy-start.2 = (bf16[512,128]{1,0:T(8,128)(2,1)S(1)}, bf16[512,128]{1,0:T(8,128)(2,1)}, u32[]{:S(2)}) copy-start(bf16[512,128]{1,0:T(8,128)(2,1)} %w_up.3) | copy-start | bytes 393220
  1.5 8.0 %collective-permute-start.1 = (bf16[4,48,128]{2,1,0:T(8,128)(2,1)S(1)}, bf16[4,48,128]{2,1,0:T(8,128)(2,1)S(1)}, u32[]{:S(2)}, u32[]{:S(2)}) collective-permute-start(bf16[4,48,128]{2,1,0:T(8,128)(2,1)S(1)} %get-tuple-element.95), channel_id=1, source_target_pairs={{16,32},{32,16},{48,64},{64,48},{80,96},{96,80},{17,33},{33,17},{4... | collective-permute-start | bytes 147464 | tf_op jit(solution)/shard_map/ppermute | solution.py:497
  2.2 8.4 %collective-permute-start = (bf16[4,48,128]{2,1,0:T(8,128)(2,1)S(1)}, bf16[4,48,128]{2,1,0:T(8,128)(2,1)S(1)}, u32[]{:S(2)}, u32[]{:S(2)}) collective-permute-start(bf16[4,48,128]{2,1,0:T(8,128)(2,1)S(1)} %get-tuple-element.96), channel_id=1, source_target_pairs={{0,16},{16,0},{32,48},{48,32},{64,80},{80,64},{96,112},{112,96},{1... | collective-permute-start | bytes 147464 | tf_op jit(solution)/shard_map/ppermute | solution.py:496
  10.6 3.9 %collective-permute-start.3 = (bf16[20,2,256]{2,1,0:T(2,128)(2,1)S(1)}, bf16[20,2,256]{2,1,0:T(2,128)(2,1)S(1)}, u32[]{:S(2)}, u32[]{:S(2)}) collective-permute-start(bf16[20,2,256]{2,1,0:T(2,128)(2,1)S(1)} %maximum_maximum_fusion.1), channel_id=1, source_target_pairs={{0,1},{1,2},{2,3},{3,4},{4,5},{5,6},{6,7},{7,8},{8,9},{9,10},{10,1... | collective-permute-start | bytes 61448 | tf_op jit(solution)/shard_map/ppermute | solution.py:513
  13.6 3.6 %collective-permute-start.2 = (bf16[20,2,256]{2,1,0:T(2,128)(2,1)S(1)}, bf16[20,2,256]{2,1,0:T(2,128)(2,1)S(1)}, u32[]{:S(2)}, u32[]{:S(2)}) collective-permute-start(bf16[20,2,256]{2,1,0:T(2,128)(2,1)S(1)} %maximum_maximum_fusion), channel_id=1, source_target_pairs={{1,0},{2,1},{3,2},{4,3},{5,4},{6,5},{7,6},{8,7},{9,8},{10,9},{11,1... | collective-permute-start | bytes 61448 | tf_op jit(solution)/shard_map/ppermute | solution.py:512
  13.8 39.2 %copy-start.3 = (s32[3]{0:T(128)}, s32[3]{0:T(128)S(1)}, u32[]{:S(2)}) copy-start(s32[3]{0:T(128)S(1)} %pad_add_fusion.pos) | copy-start | bytes 40
  22.2 23.0 %all-to-all-start = ((bf16[64,24,128]{2,1,0:T(8,128)(2,1)}), bf16[64,24,128]{2,1,0:T(8,128)(2,1)S(1)}, u32[]{:S(2)}, u32[]{:S(2)}) async-start(bf16[64,24,128]{2,1,0:T(8,128)(2,1)} %get-tuple-element.47), calls=%async_computation | async-start | bytes 786432 | tf_op jit(solution)/shard_map/all_to_all | solution.py:555
  45.3 16.4 %copy-start = (bf16[64,24,128]{2,1,0:T(8,128)(2,1)}, bf16[64,24,128]{2,1,0:T(8,128)(2,1)S(1)}, u32[]{:S(2)}) copy-start(bf16[64,24,128]{2,1,0:T(8,128)(2,1)S(1)} %all-to-all-done) | copy-start | bytes 1179652
  45.3 1.7 %collective-permute-start.4 = (bf16[1536,128]{1,0:T(8,128)(2,1)S(1)}, bf16[1536,128]{1,0:T(8,128)(2,1)S(1)}, u32[]{:S(2)}, u32[]{:S(2)}) collective-permute-start(bf16[1536,128]{1,0:T(8,128)(2,1)S(1)} %bitcast.17), channel_id=1, source_target_pairs={{0,1},{1,0},{2,3},{3,2},{4,5},{5,4},{6,7},{7,6},{8,9},{9,8},{10,11... | collective-permute-start | bytes 1179656 | tf_op jit(solution)/shard_map/ppermute | solution.py:570
  47.0 14.6 %copy-start.1 = (bf16[1536,128]{1,0:T(8,128)(2,1)}, bf16[1536,128]{1,0:T(8,128)(2,1)S(1)}, u32[]{:S(2)}) copy-start(bf16[1536,128]{1,0:T(8,128)(2,1)S(1)} %collective-permute-done.4.every_far.every_far_out) | copy-start | bytes 1179652
  53.0 1.9 %collective-permute-start.5 = (bf16[1152,128]{1,0:T(8,128)(2,1)}, bf16[1152,128]{1,0:T(8,128)(2,1)S(1)}, u32[]{:S(2)}, u32[]{:S(2)}) collective-permute-start(bf16[1152,128]{1,0:T(8,128)(2,1)} %get-tuple-element.59), channel_id=1, source_target_pairs={{0,1},{1,0},{2,3},{3,2},{4,5},{5,4},{6,7},{7,6},{8,9},{9,8},{10,11... | collective-permute-start | bytes 884744 | tf_op jit(solution)/shard_map/ppermute | solution.py:602
  56.7 14.7 %all-to-all-start.1 = ((bf16[64,9,2,128]{3,2,1,0:T(2,128)(2,1)}), bf16[64,9,2,128]{3,2,1,0:T(2,128)(2,1)S(1)}, u32[]{:S(2)}, u32[]{:S(2)}) async-start(bf16[64,9,2,128]{3,2,1,0:T(2,128)(2,1)} %bitcast.8), calls=%async_computation.1 | async-start | bytes 589824 | tf_op jit(solution)/shard_map/all_to_all | solution.py:613
  72.7 23.8 %all-to-all-start.2 = ((bf16[128,9,2,128]{3,2,1,0:T(2,128)(2,1)}), bf16[128,9,2,128]{3,2,1,0:T(2,128)(2,1)S(1)}, u32[]{:S(2)}, u32[]{:S(2)}) async-start(bf16[128,9,2,128]{3,2,1,0:T(2,128)(2,1)} %bitcast.10), calls=%async_computation.2 | async-start | bytes 1179648 | tf_op jit(solution)/shard_map/all_to_all | solution.py:643

commit v4 on v3

--- a/solution.py
+++ b/solution.py
@@ -170,8 +170,8 @@
 
 def second_kernel(
     pos, every, every_far, w_up, w_eff_far, hid_far, slope_far, dm_far, field_far, grad_far,
-    keep_out, give_out, merged_out, dact_out,
-    keep, give, w_eff, hid, slope, dm, field, own_grad, fine_cat, merged_cat, merged_here, dact_here, sems,
+    parts_out, merged_out, dact_out,
+    parts, w_eff, hid, slope, dm, field, own_grad, fine_cat, merged_cat, merged_here, dact_here, sems,
 ):
     lat, lon, core = pos[0], pos[1], pos[2]
     fetches = [
@@ -190,8 +190,8 @@
     stores = [
         pltpu.make_async_copy(merged_here, merged_out, sems.at[6]),
         pltpu.make_async_copy(dact_here, dact_out, sems.at[7]),
-        pltpu.make_async_copy(give, give_out, sems.at[8]),
-        pltpu.make_async_copy(keep, keep_out, sems.at[9]),
+        pltpu.make_async_copy(parts.at[0:HALF, :], parts_out.at[0:HALF, :], sems.at[8]),
+        pltpu.make_async_copy(parts.at[HALF:, :], parts_out.at[HALF:, :], sems.at[9]),
     ]
     for fetch in fetches:
         fetch.start()
@@ -274,16 +274,17 @@
     center = dact_here[2 * STRIDE : 2 * STRIDE + OWN, :]
     own_dact = jnp.where(slot < COLS, center, jnp.zeros_like(center))
     center_grad = own_grad[...].reshape(OWN, DEPTH)
-    zero = core == 0
     for tap in range(3):
-        rows = slice(tap * 384, tap * 384 + 384)
         start = (tap + 1) * STRIDE
-        dec = mm(merged_cat[start : start + OWN, :], center_grad, ((0,), (0,))).astype(BF16)
+        parts[tap * 384 : tap * 384 + 384, :] = mm(
+            merged_cat[start : start + OWN, :], center_grad, ((0,), (0,))
+        ).astype(BF16)
+    stores[2].start()
+    for tap in range(3):
         start = (tap + 2) * STRIDE
-        enc = mm(fine_cat[start : start + OWN, :], own_dact, ((0,), (0,))).astype(BF16)
-        give[rows, :] = jnp.where(zero, enc, dec)
-        keep[rows, :] = jnp.where(zero, dec, enc)
-    stores[2].start()
+        parts[HALF + tap * 384 : HALF + tap * 384 + 384, :] = mm(
+            fine_cat[start : start + OWN, :], own_dact, ((0,), (0,))
+        ).astype(BF16)
     stores[3].start()
     for store in stores:
         store.wait()
@@ -377,33 +378,19 @@
     return value - 18 * ((value * 3641) >> 16)
 
 
-def add_kernel(got, keep_far, out, keep, sems):
-    fetch = pltpu.make_async_copy(keep_far, keep, sems.at[0])
-    fetch.start()
-    fetch.wait()
-    out[...] = (keep[...].astype(F32) + got[...].astype(F32)).astype(BF16)
-
-
 def fold_kernel(spread, out):
-    slot = remainder(lax.broadcasted_iota(jnp.int32, (32, HALF), 1))
-    pick = slot == lax.broadcasted_iota(jnp.int32, (32, HALF), 0)
+    full = 2 * HALF
+    slot = remainder(lax.broadcasted_iota(jnp.int32, (32, full), 1))
+    pick = slot == lax.broadcasted_iota(jnp.int32, (32, full), 0)
     total = mm(pick.astype(F32).astype(BF16), spread[...]).astype(BF16)
-    slot = remainder(lax.broadcasted_iota(jnp.int32, (2 * HALF, 1), 0))
-    copy = lax.broadcasted_iota(jnp.int32, (2 * HALF, 32), 1) == slot
+    slot = remainder(lax.broadcasted_iota(jnp.int32, (full, 1), 0))
+    copy = lax.broadcasted_iota(jnp.int32, (full, 32), 1) == slot
     out[...] = mm(copy.astype(F32).astype(BF16), total).astype(BF16)
 
 
 def finish_kernel(whole, g_dec, g_enc):
-    row = lax.broadcasted_iota(jnp.int32, (144, 1), 0)
-    half = (row >= 72).astype(jnp.int32)
-    rest = row - 72 * half
-    step = sum((rest >= 18 * k).astype(jnp.int32) for k in (1, 2, 3))
-    src = rest + 18 * step + 18 * half
-    order = (lax.broadcasted_iota(jnp.int32, (144, 144), 1) == src).astype(F32).astype(BF16)
-    for block in range(16):
-        rows = mm(order, whole[144 * block : 144 * block + 144, :])
-        g_dec[72 * block : 72 * block + 72, :] = rows[:72]
-        g_enc[72 * block : 72 * block + 72, :] = rows[72:]
+    g_dec[...] = whole[:HALF].astype(F32)
+    g_enc[...] = whole[HALF:].astype(F32)
 
 
 def tail_kernel(
@@ -568,19 +555,17 @@
     )(early, held(w_bot.reshape(9, WIDE, WIDE))).reshape(9 * DEPTH, WIDE)
     every, w_eff = lax.optimization_barrier((every, w_eff))
     every_far = lax.ppermute(every, "core", swap)
-    keep, give, merged, dact = pl.pallas_call(
+    parts, merged, dact = pl.pallas_call(
         second_kernel,
         in_specs=[smem(), vmem(), vmem(), vmem()] + [far()] * 6,
-        out_specs=[far()] * 4,
+        out_specs=[far()] * 3,
         out_shape=[
-            pltpu.HBM((HALF, DEPTH), BF16),
-            pltpu.HBM((HALF, DEPTH), BF16),
+            pltpu.HBM((2 * HALF, DEPTH), BF16),
             pltpu.HBM((RIM, DEPTH), BF16),
             pltpu.HBM((RIM, DEPTH), BF16),
         ],
         scratch_shapes=[
-            pltpu.VMEM((HALF, DEPTH), BF16),
-            pltpu.VMEM((HALF, DEPTH), BF16),
+            pltpu.VMEM((2 * HALF, DEPTH), BF16),
             pltpu.VMEM((9 * DEPTH, WIDE), BF16),
             pltpu.VMEM((RIM, DEPTH), BF16),
             pltpu.VMEM((RIM, DEPTH), F32),
@@ -596,21 +581,10 @@
         name="second",
         compiler_params=grant(30),
     )(pos, every, every_far, w_up, *(held(x) for x in (w_eff, hid, slope, dm, field, grad)))
-    keep, give, every, every_far, merged, dact = lax.optimization_barrier(
-        (keep, give, every, every_far, merged, dact)
-    )
-    got = lax.ppermute(give, "core", swap)
-    half = pl.pallas_call(
-        add_kernel,
-        in_specs=[vmem(), far()],
-        out_specs=vmem(),
-        out_shape=shape((HALF, DEPTH), BF16),
-        scratch_shapes=[pltpu.VMEM((HALF, DEPTH), BF16), pltpu.SemaphoreType.DMA((1,))],
-        name="add",
-        compiler_params=grant(6),
-    )(got, held(keep))
-    half, every, every_far = lax.optimization_barrier((half, every, every_far))
-    spread = lax.all_to_all(half.reshape(COUNT, 9, 2, DEPTH), PEERS, 0, 0)
+    parts, every, every_far, merged, dact = lax.optimization_barrier(
+        (parts, every, every_far, merged, dact)
+    )
+    spread = lax.all_to_all(parts.reshape(2 * COUNT, 9, 2, DEPTH), EVERYONE, 0, 0)
     table, g_up = pl.pallas_call(
         coarse_kernel,
         in_specs=[smem(), vmem(), far(), far(), far()],
@@ -638,7 +612,7 @@
         out_shape=pltpu.VMEM((2 * HALF, DEPTH), BF16),
         name="fold",
         compiler_params=grant(8),
-    )(spread.reshape(HALF, DEPTH))
+    )(spread.reshape(2 * HALF, DEPTH))
     total, table, merged, dact = lax.optimization_barrier((total, table, merged, dact))
     whole = lax.all_to_all(total.reshape(2 * COUNT, 9, 2, DEPTH), EVERYONE, 0, 0)
     g_bot, block_out, field_grad, g_down = pl.pallas_call(

time: 98.4 us -> 93.5 us (0.950)
  starting transfers between devices: 36.3 us -> 30.3 us
  waiting for transfers between devices: 21.2 us -> 24.6 us
  Pallas kernels: 37.6 us -> 35.2 us
    all_to_all x1, waiting for transfers between devices: 0.31 us -> 5.22 us  [body(): lax.all_to_all(parts.reshape(2 * COUNT, 9, 2, DEPTH), EVERYONE, 0, 0)]
    all_to_all x1, starting transfers between devices: 9.11 us -> 4.56 us  [body(): lax.all_to_all(total.reshape(2 * COUNT, 9, 2, DEPTH), EVERYONE, 0, 0)]
    pallas_call x1 -> x0, Pallas kernels: 1.75 us -> none  [body(): pl.pallas_call(add_kernel, in_specs=[vmem(), far()], out_specs=vmem(), ou...]
    ppermute x1 -> x0, waiting for transfers between devices: 1.42 us -> none  [body(): got = lax.ppermute(give, 'core', swap)]
  transfers between devices with their start and end apart: 9 -> 8, of which waited for: 8 -> 7; matrix products, arithmetic and copies ran while one was open for 1% -> 1% of each run, Pallas kernels for 23% -> 24%
where the time goes in v4:
time: 93.5 us; the launch traced here: 93 us
  Pallas kernels  35.2 us (38%)
  starting transfers between devices  30.3 us (32%)
  waiting for transfers between devices  24.6 us (26%)
  local copies, waits for them, and re-layouts  1.78 us (2%)
    all_to_all x1, starting transfers between devices, body(): every = lax.all_to_all(pack, PEERS, 0, 0).reshape(COUNT * PACK, DEPTH)  11.2 us
    pallas_call x1, Pallas kernels, body(): pl.pallas_call(coarse_kernel, in_specs=[smem(), vmem(), far(), far(), far...  9.38 us
    pallas_call x1, Pallas kernels, body(): pl.pallas_call(tail_kernel, in_specs=[vmem()] + [far()] * 6, out_specs=[f...  7.89 us
    all_to_all x1, waiting for transfers between devices, body(): every = lax.all_to_all(pack, PEERS, 0, 0).reshape(COUNT * PACK, DEPTH)  6.97 us
    all_to_all x1, waiting for transfers between devices, body(): lax.all_to_all(total.reshape(2 * COUNT, 9, 2, DEPTH), EVERYONE, 0, 0)  6.74 us
    ppermute x1, starting transfers between devices, body(): got_inner = lax.ppermute(jnp.where(even, under, over), 'lat', inner)  6.47 us
    pallas_call x1, Pallas kernels, body(): pl.pallas_call(second_kernel, in_specs=[smem(), vmem(), vmem(), vmem()] +...  5.64 us
    all_to_all x1, waiting for transfers between devices, body(): lax.all_to_all(parts.reshape(2 * COUNT, 9, 2, DEPTH), EVERYONE, 0, 0)  5.22 us
  transfers between devices with their start and end apart: 8, of which 7 were waited for; matrix products, arithmetic and copies ran while one was open for 1% of the time, Pallas kernels for 24%

profile of v4, /device:TPU:1, one launch (start us, length us, event | category | flops | bytes accessed | tf_op | source)
XLA Modules:
  0.0 93.0 jit_solution(16257428954030164965)
XLA Ops:
  0.7 0.8 fusion.6
  1.5 0.7 collective-permute-start.1
  2.2 6.5 %collective-permute-start = (bf16[4,48,128]{2,1,0:T(8,128)(2,1)S(1)}, bf16[4,48,128]{2,1,0:T(8,128)(2,1)S(1)}, u32[]{:S(2)}, u32[]{:S(2)}) collective-permute-start(bf16[4,48,128]{2,1,0:T(8,128)(2,1)S(1)} %get-tuple-element.86), channel_id=1, source_target_pairs={{0,16},{16,0},{32,48},{48,32},{64,80},{80,64},{96,112},{112,96},{1... | collective-permute-start | bytes 147464 | tf_op jit(solution)/shard_map/ppermute | solution.py:483
  8.6 0.8 fusion.4
  9.5 1.0 %collective-permute-done.got_inner = bf16[4,48,128]{2,1,0:T(8,128)(2,1)S(1)} collective-permute-done((bf16[4,48,128]{2,1,0:T(8,128)(2,1)S(1)}, bf16[4,48,128]{2,1,0:T(8,128)(2,1)S(1)}, u32[]{:S(2)}, u32[]{:S(2)}) %collective-permute-start) | collective-permute-done | bytes 49184 | tf_op jit(solution)/shard_map/ppermute | solution.py:483
  10.6 3.0 %collective-permute-start.3 = (bf16[20,2,256]{2,1,0:T(2,128)(2,1)S(1)}, bf16[20,2,256]{2,1,0:T(2,128)(2,1)S(1)}, u32[]{:S(2)}, u32[]{:S(2)}) collective-permute-start(bf16[20,2,256]{2,1,0:T(2,128)(2,1)S(1)} %maximum_maximum_fusion.1), channel_id=1, source_target_pairs={{0,1},{1,2},{2,3},{3,4},{4,5},{5,6},{6,7},{7,8},{8,9},{9,10},{10,1... | collective-permute-start | bytes 61448 | tf_op jit(solution)/shard_map/ppermute | solution.py:500
  13.9 0.6 collective-permute-done.3
  14.5 2.7 %collective-permute-done.2 = bf16[20,2,256]{2,1,0:T(2,128)(2,1)S(1)} collective-permute-done((bf16[20,2,256]{2,1,0:T(2,128)(2,1)S(1)}, bf16[20,2,256]{2,1,0:T(2,128)(2,1)S(1)}, u32[]{:S(2)}, u32[]{:S(2)}) %collective-permute-start.2) | collective-permute-done | bytes 20512 | tf_op jit(solution)/shard_map/ppermute | solution.py:499
  17.2 0.1 fusion.2.strip
  17.3 4.9 %first.1 = (bf16[64,24,128]{2,1,0:T(8,128)(2,1)}, bf16[1216,128]{1,0:T(8,128)(2,1)}, f32[1216,128]{1,0:T(8,128)}, f32[1216,128]{1,0:T(8,128)}, bf16[21,64,128]{2,1,0:T(8,128)(2,1)}) custom-call(s32[3]{0:T(128)S(1)} %pad_add_fusion.pos, bf16[4,48,128]{2,1,0:T(8,128)(2,1)S(1)} %collective-permute-done.got_inner, ...), custom_call_target="tpu_custom_call" | custom-call | tf_op jit(solution)/shard_map/first/pallas_call | solution.py:511
  22.2 11.2 %all-to-all-start = ((bf16[64,24,128]{2,1,0:T(8,128)(2,1)}), bf16[64,24,128]{2,1,0:T(8,128)(2,1)S(1)}, u32[]{:S(2)}, u32[]{:S(2)}) async-start(bf16[64,24,128]{2,1,0:T(8,128)(2,1)} %get-tuple-element.42), calls=%async_computation | async-start | bytes 786432 | tf_op jit(solution)/shard_map/all_to_all | solution.py:542
  33.4 4.9 %weights.1 = bf16[9,128,512]{2,1,0:T(8,128)(2,1)} custom-call(bf16[128,512]{1,0:T(8,128)(2,1)} %w_down.2, bf16[9,512,512]{2,1,0:T(8,128)(2,1)} %bitcast.22), custom_call_target="tpu_custom_call" | custom-call | tf_op jit(solution)/shard_map/weights/pallas_call | solution.py:543
  38.3 7.0 %all-to-all-done = bf16[64,24,128]{2,1,0:T(8,128)(2,1)S(1)} async-done(((bf16[64,24,128]{2,1,0:T(8,128)(2,1)}), bf16[64,24,128]{2,1,0:T(8,128)(2,1)S(1)}, u32[]{:S(2)}, u32[]{:S(2)}) %all-to-all-start) | async-done | bytes 393248 | tf_op jit(solution)/shard_map/all_to_all | solution.py:542
  45.3 0.4 collective-permute-start.4
  45.7 1.3 %collective-permute-done.4.every_far.every_far_out = bf16[1536,128]{1,0:T(8,128)(2,1)S(1)} collective-permute-done((bf16[1536,128]{1,0:T(8,128)(2,1)S(1)}, bf16[1536,128]{1,0:T(8,128)(2,1)S(1)}, u32[]{:S(2)}, u32[]{:S(2)}) %collective-permute-start.4) | collective-permute-done | bytes 393248 | tf_op jit(solution)/shard_map/ppermute | solution.py:557
  47.0 5.6 %second.1 = (bf16[2304,128]{1,0:T(8,128)(2,1)}, bf16[1216,128]{1,0:T(8,128)(2,1)}, bf16[1216,128]{1,0:T(8,128)(2,1)}) custom-call(s32[3]{0:T(128)S(1)} %pad_add_fusion.pos, bf16[1536,128]{1,0:T(8,128)(2,1)S(1)} %bitcast.18, bf16[1536,128]{1,0:T(8,128)(2,1)S(1)} %collective-permute-done.4.every_far.every_far_out, bf16[512,128]{1,0:T(8,128)(2,1)S(1)} %copy-done.2, ...), custom_call_target="tpu_custom_call" | custom-call | tf_op jit(solution)/shard_map/second/pallas_call | solution.py:558
  52.7 4.0 %all-to-all-start.1 = ((bf16[128,9,2,128]{3,2,1,0:T(2,128)(2,1)}), bf16[128,9,2,128]{3,2,1,0:T(2,128)(2,1)S(1)}, u32[]{:S(2)}, u32[]{:S(2)}) async-start(bf16[128,9,2,128]{3,2,1,0:T(2,128)(2,1)} %bitcast.30), calls=%async_computation.1 | async-start | bytes 1179648 | tf_op jit(solution)/shard_map/all_to_all | solution.py:587
  56.7 9.4 %coarse.1 = (bf16[9,128,512]{2,1,0:T(8,128)(2,1)}, f32[512,128]{1,0:T(8,128)}) custom-call(s32[3]{0:T(128)} %copy-done.3, bf16[512,128]{1,0:T(8,128)(2,1)} %w_up.3, bf16[1536,128]{1,0:T(8,128)(2,1)} %bitcast.19, bf16[1536,128]{1,0:T(8,128)(2,1)} %copy-done.1, bf16[1152,512]{1,0:T(8,128)(2,1)} %bitcast.25), custom_call_target="tpu_custom_call" | custom-call | tf_op jit(solution)/shard_map/coarse/pallas_call | solution.py:588
  66.1 5.2 %all-to-all-done.1 = bf16[128,9,2,128]{3,2,1,0:T(2,128)(2,1)S(1)} async-done(((bf16[128,9,2,128]{3,2,1,0:T(2,128)(2,1)}), bf16[128,9,2,128]{3,2,1,0:T(2,128)(2,1)S(1)}, u32[]{:S(2)}, u32[]{:S(2)}) %all-to-all-start.1) | async-done | bytes 589856 | tf_op jit(solution)/shard_map/all_to_all | solution.py:587
  71.3 1.4 %fold.1 = bf16[2304,128]{1,0:T(8,128)(2,1)} custom-call(bf16[2304,128]{1,0:T(8,128)(2,1)S(1)} %bitcast.21), custom_call_target="tpu_custom_call" | custom-call | tf_op jit(solution)/shard_map/fold/pallas_call | solution.py:608
  72.7 4.6 %all-to-all-start.2 = ((bf16[128,9,2,128]{3,2,1,0:T(2,128)(2,1)}), bf16[128,9,2,128]{3,2,1,0:T(2,128)(2,1)S(1)}, u32[]{:S(2)}, u32[]{:S(2)}) async-start(bf16[128,9,2,128]{3,2,1,0:T(2,128)(2,1)} %bitcast.10), calls=%async_computation.2 | async-start | bytes 1179648 | tf_op jit(solution)/shard_map/all_to_all | solution.py:617
  77.3 7.9 %tail.1 = (f32[9,512,512]{2,1,0:T(8,128)}, bf16[16,48,128]{2,1,0:T(8,128)(2,1)}, bf16[16,48,128]{2,1,0:T(8,128)(2,1)}, f32[128,512]{1,0:T(8,128)}) custom-call(bf16[128,512]{1,0:T(8,128)(2,1)} %w_down.2, bf16[9,128,512]{2,1,0:T(8,128)(2,1)} %get-tuple-element.62.table_far, bf16[1216,128]{1,0:T(8,128)(2,1)} %get-tuple-element.63.merged_far, ...), custom_call_target="tpu_custom_call" | custom-call | tf_op jit(solution)/shard_map/tail/pallas_call | solution.py:618
  85.2 6.7 %all-to-all-done.2 = bf16[128,9,2,128]{3,2,1,0:T(2,128)(2,1)S(1)} async-done(((bf16[128,9,2,128]{3,2,1,0:T(2,128)(2,1)}), bf16[128,9,2,128]{3,2,1,0:T(2,128)(2,1)S(1)}, u32[]{:S(2)}, u32[]{:S(2)}) %all-to-all-start.2) | async-done | bytes 589856 | tf_op jit(solution)/shard_map/all_to_all | solution.py:617
  91.9 1.0 %finish.1 = (f32[1152,128]{1,0:T(8,128)}, f32[1152,128]{1,0:T(8,128)}) custom-call(bf16[2304,128]{1,0:T(8,128)(2,1)S(1)} %bitcast.20), custom_call_target="tpu_custom_call" | custom-call | tf_op jit(solution)/shard_map/finish/pallas_call | solution.py:655
  (19 shorter events, 0.3 us)
Async XLA Ops:
  0.6 46.4 %copy-start.2 = (bf16[512,128]{1,0:T(8,128)(2,1)S(1)}, bf16[512,128]{1,0:T(8,128)(2,1)}, u32[]{:S(2)}) copy-start(bf16[512,128]{1,0:T(8,128)(2,1)} %w_up.3) | copy-start | bytes 393220
  1.5 8.0 %collective-permute-start.1 = (bf16[4,48,128]{2,1,0:T(8,128)(2,1)S(1)}, bf16[4,48,128]{2,1,0:T(8,128)(2,1)S(1)}, u32[]{:S(2)}, u32[]{:S(2)}) collective-permute-start(bf16[4,48,128]{2,1,0:T(8,128)(2,1)S(1)} %get-tuple-element.85), channel_id=1, source_target_pairs={{16,32},{32,16},{48,64},{64,48},{80,96},{96,80},{17,33},{33,17},{4... | collective-permute-start | bytes 147464 | tf_op jit(solution)/shard_map/ppermute | solution.py:484
  2.2 8.4 %collective-permute-start = (bf16[4,48,128]{2,1,0:T(8,128)(2,1)S(1)}, bf16[4,48,128]{2,1,0:T(8,128)(2,1)S(1)}, u32[]{:S(2)}, u32[]{:S(2)}) collective-permute-start(bf16[4,48,128]{2,1,0:T(8,128)(2,1)S(1)} %get-tuple-element.86), channel_id=1, source_target_pairs={{0,16},{16,0},{32,48},{48,32},{64,80},{80,64},{96,112},{112,96},{1... | collective-permute-start | bytes 147464 | tf_op jit(solution)/shard_map/ppermute | solution.py:483
  10.6 3.9 %collective-permute-start.3 = (bf16[20,2,256]{2,1,0:T(2,128)(2,1)S(1)}, bf16[20,2,256]{2,1,0:T(2,128)(2,1)S(1)}, u32[]{:S(2)}, u32[]{:S(2)}) collective-permute-start(bf16[20,2,256]{2,1,0:T(2,128)(2,1)S(1)} %maximum_maximum_fusion.1), channel_id=1, source_target_pairs={{0,1},{1,2},{2,3},{3,4},{4,5},{5,6},{6,7},{7,8},{8,9},{9,10},{10,1... | collective-permute-start | bytes 61448 | tf_op jit(solution)/shard_map/ppermute | solution.py:500
  13.6 3.6 %collective-permute-start.2 = (bf16[20,2,256]{2,1,0:T(2,128)(2,1)S(1)}, bf16[20,2,256]{2,1,0:T(2,128)(2,1)S(1)}, u32[]{:S(2)}, u32[]{:S(2)}) collective-permute-start(bf16[20,2,256]{2,1,0:T(2,128)(2,1)S(1)} %maximum_maximum_fusion), channel_id=1, source_target_pairs={{1,0},{2,1},{3,2},{4,3},{5,4},{6,5},{7,6},{8,7},{9,8},{10,9},{11,1... | collective-permute-start | bytes 61448 | tf_op jit(solution)/shard_map/ppermute | solution.py:499
  13.8 38.9 %copy-start.3 = (s32[3]{0:T(128)}, s32[3]{0:T(128)S(1)}, u32[]{:S(2)}) copy-start(s32[3]{0:T(128)S(1)} %pad_add_fusion.pos) | copy-start | bytes 40
  22.2 23.0 %all-to-all-start = ((bf16[64,24,128]{2,1,0:T(8,128)(2,1)}), bf16[64,24,128]{2,1,0:T(8,128)(2,1)S(1)}, u32[]{:S(2)}, u32[]{:S(2)}) async-start(bf16[64,24,128]{2,1,0:T(8,128)(2,1)} %get-tuple-element.42), calls=%async_computation | async-start | bytes 786432 | tf_op jit(solution)/shard_map/all_to_all | solution.py:542
  45.3 11.4 %copy-start = (bf16[64,24,128]{2,1,0:T(8,128)(2,1)}, bf16[64,24,128]{2,1,0:T(8,128)(2,1)S(1)}, u32[]{:S(2)}) copy-start(bf16[64,24,128]{2,1,0:T(8,128)(2,1)S(1)} %all-to-all-done) | copy-start | bytes 1179652
  45.3 1.7 %collective-permute-start.4 = (bf16[1536,128]{1,0:T(8,128)(2,1)S(1)}, bf16[1536,128]{1,0:T(8,128)(2,1)S(1)}, u32[]{:S(2)}, u32[]{:S(2)}) collective-permute-start(bf16[1536,128]{1,0:T(8,128)(2,1)S(1)} %bitcast.17), channel_id=1, source_target_pairs={{0,1},{1,0},{2,3},{3,2},{4,5},{5,4},{6,7},{7,6},{8,9},{9,8},{10,11... | collective-permute-start | bytes 1179656 | tf_op jit(solution)/shard_map/ppermute | solution.py:557
  47.0 9.7 %copy-start.1 = (bf16[1536,128]{1,0:T(8,128)(2,1)}, bf16[1536,128]{1,0:T(8,128)(2,1)S(1)}, u32[]{:S(2)}) copy-start(bf16[1536,128]{1,0:T(8,128)(2,1)S(1)} %collective-permute-done.4.every_far.every_far_out) | copy-start | bytes 1179652
  52.7 18.6 %all-to-all-start.1 = ((bf16[128,9,2,128]{3,2,1,0:T(2,128)(2,1)}), bf16[128,9,2,128]{3,2,1,0:T(2,128)(2,1)S(1)}, u32[]{:S(2)}, u32[]{:S(2)}) async-start(bf16[128,9,2,128]{3,2,1,0:T(2,128)(2,1)} %bitcast.30), calls=%async_computation.1 | async-start | bytes 1179648 | tf_op jit(solution)/shard_map/all_to_all | solution.py:587
  72.7 19.2 %all-to-all-start.2 = ((bf16[128,9,2,128]{3,2,1,0:T(2,128)(2,1)}), bf16[128,9,2,128]{3,2,1,0:T(2,128)(2,1)S(1)}, u32[]{:S(2)}, u32[]{:S(2)}) async-start(bf16[128,9,2,128]{3,2,1,0:T(2,128)(2,1)} %bitcast.10), calls=%async_computation.2 | async-start | bytes 1179648 | tf_op jit(solution)/shard_map/all_to_all | solution.py:617
